TPU v7x, 32 devices: a whole 2x2x4 slice. The times are simulated.
32 devices in a mesh: dp: 4 (over x, y), cp: 8 (over z, core).
Axes of the slice: x: 2, y: 2, z: 4, core: 2. Of those that a mesh axis runs over, the one named last changes fastest.
Arguments:
- q: bfloat16 [32768, 4, 128], P(('dp', 'cp')), parts along dimension 0
- k: bfloat16 [32768, 4, 128], P(('dp', 'cp')), parts along dimension 0
- v: bfloat16 [32768, 4, 128], P(('dp', 'cp')), parts along dimension 0
- o: bfloat16 [32768, 4, 128], P(('dp', 'cp')), parts along dimension 0
- do: bfloat16 [32768, 4, 128], P(('dp', 'cp')), parts along dimension 0
- lse: float32 [4, 32768], P(None, ('dp', 'cp')), parts along dimension 1
Outputs:
- output 1: bfloat16 [32768, 4, 128], P(('dp', 'cp')), parts along dimension 0
- output 2: bfloat16 [32768, 4, 128], P(('dp', 'cp')), parts along dimension 0
- output 3: bfloat16 [32768, 4, 128], P(('dp', 'cp')), parts along dimension 0
There are 4 independent parts. A program takes and returns all parts, laid end to end along the dimension named above; each array names one.
All inputs are finite; a program needn't handle non-finite values.
Results may differ from a plain program's by a relative error of at most 0.001.
Values are sent between devices in bfloat16 or wider.
A program may use at most 1 GiB of HBM per device.

v0:
```python
import jax
import jax.numpy as jnp
from jax import lax
from jax.sharding import PartitionSpec as P


def solution(mesh):
    ncp = mesh.shape['cp']
    f32, bf16 = jnp.float32, jnp.bfloat16
    rows = P(('dp', 'cp'))
    cols = P(None, ('dp', 'cp'))
    perm = [(p, (p + 1) % ncp) for p in range(ncp)]

    def shift(x):
        return lax.ppermute(x, 'cp', perm)

    def local(q, k, v, o, do, lse):
        n, h, d = q.shape
        kh = k.shape[1]
        g = h // kh
        scale = d ** -0.5
        me = lax.axis_index('cp')
        qs = q.reshape(n, kh, g, d)
        dos = do.reshape(n, kh, g, d)
        delta = jnp.sum(do.astype(f32) * o.astype(f32), axis=-1)
        delta = jnp.transpose(delta.reshape(n, kh, g), (1, 2, 0))[..., None]
        lses = lse.reshape(kh, g, n)[..., None]
        qpos = jnp.arange(n)[:, None] * ncp + me
        dq = jnp.zeros((n, kh, g, d), f32)
        dk = jnp.zeros((n, kh, d), f32)
        dv = jnp.zeros((n, kh, d), f32)
        for step in range(ncp):
            src = (me - step) % ncp
            mask = qpos >= jnp.arange(n)[None, :] * ncp + src
            s = jnp.einsum('ikgd,jkd->kgij', qs, k, preferred_element_type=f32) * scale
            pr = jnp.exp(jnp.where(mask, s - lses, -jnp.inf))
            dv = dv + jnp.einsum('kgij,ikgd->jkd', pr.astype(bf16), dos, preferred_element_type=f32)
            dp = jnp.einsum('ikgd,jkd->kgij', dos, v, preferred_element_type=f32)
            ds = (pr * (dp - delta)).astype(bf16)
            dq = dq + jnp.einsum('kgij,jkd->ikgd', ds, k, preferred_element_type=f32)
            dk = dk + jnp.einsum('kgij,ikgd->jkd', ds, qs, preferred_element_type=f32)
            if step < ncp - 1:
                k = shift(k)
                v = shift(v)
            dk = shift(dk)
            dv = shift(dv)
        return ((dq * scale).reshape(n, h, d).astype(bf16),
                (dk * scale).astype(bf16),
                dv.astype(bf16))

    return jax.shard_map(local, mesh=mesh,
                         in_specs=(rows, rows, rows, rows, rows, cols),
                         out_specs=(rows, rows, rows), check_vma=False)
```

profile of v0, /device:TPU:0, one launch (start us, length us, event | category | flops | bytes accessed | tf_op | source)
XLA Modules:
  0.0 576.6 jit_solution(14187747200623734464)
XLA Ops:
  8.6 2.7 multiply_reduce_fusion
  11.5 9.4 %fusion.130 = f32[4,1024,1024]{2,1,0:T(8,128)} fusion(bf16[1024,4,128]{2,1,0:T(4,128)(2,1)} %param.7, bf16[1024,4,128]{2,1,0:T(4,128)(2,1)S(1)} %copy-done), kind=kOutput, calls=%fused_computation.168 | convolution fusion | flops 1073741824 | bytes 18874368 | tf_op jit(solution)/shard_map/ikgd,jkd->kgij/dot_general | solution.py:35
  21.0 6.5 %broadcast_compare_fusion.6 = (pred[1024,1024]{0,1:T(8,128)(4,1)}, pred[1024,1024]{0,1:T(8,128)(4,1)}, pred[1024,1024]{0,1:T(8,128)(4,1)}, pred[1024,1024]{0,1:T...) fusion(s32[1024]{0:T(1024)S(1)} %fusion.111, ...), kind=kLoop, calls=%fused_computation.135 | loop fusion | flops 8388608 | bytes 8425472 | tf_op jit(solution)/shard_map/ge | solution.py:34
  27.5 9.6 %fusion.14 = bf16[4,1,1024,1024]{2,3,0,1:T(8,128)(2,1)S(1)} fusion(f32[4,1024,1024]{2,1,0:T(8,128)} %fusion.130, f32[4,1024]{1,0:T(4,128)S(1)} %copy.61, f32[4,1024]{1,0:T(4,128)S(1)} %copy-done.26, pred[1024,1024]{0,1:T(8,128)(4,1)S(1)} %get-tuple-element.16, bf16[1024,4,128]{2,1,0:T(4,128)(2,1)S(1)} %copy-done.14, bf16[1024,4,128]{2,1,0:T(4,128)(2,1)S(1)} %copy-done.15), kind=kOutput, calls=%fused_computation.43 | convolution fusion | flops 1098907648 | bytes 28344320 | tf_op jit(solution)/shard_map/ikgd,jkd->kgij/dot_general | solution.py:38
  37.0 3.3 copy-done.3
  40.3 3.6 fusion.93
  44.2 11.7 %fusion.90 = f32[1024,4,128]{2,0,1:T(8,128)} fusion(f32[4,1024,1024]{2,1,0:T(8,128)} %fusion.130, f32[4,1024]{1,0:T(4,128)S(1)} %copy-done.26, pred[1024,1024]{0,1:T(8,128)(4,1)} %copy-done.24, bf16[1024,4,128]{2,1,0:T(4,128)(2,1)} %param.10), kind=kOutput, calls=%fused_computation.137 | convolution fusion | flops 1090519040 | bytes 20987904 | tf_op jit(solution)/shard_map/kgij,ikgd->jkd/dot_general | solution.py:37
  57.5 7.7 %fusion.62 = f32[4,1024,128]{2,1,0:T(8,128)} fusion(bf16[4,1,1024,1024]{2,3,0,1:T(8,128)(2,1)} %copy-done.3, bf16[1024,4,128]{2,1,0:T(4,128)(2,1)S(1)} %copy-done.1), kind=kOutput, calls=%fused_computation.94 | convolution fusion | flops 1073741824 | bytes 11534336 | tf_op jit(solution)/shard_map/kgij,jkd->ikgd/dot_general | solution.py:40
  65.3 8.1 %fusion.168 = f32[4,1024,1024]{2,1,0:T(8,128)} fusion(bf16[1024,4,128]{2,0,1:T(8,128)(2,1)S(1)} %collective-permute-done, bf16[1024,4,128]{2,1,0:T(4,128)(2,1)S(1)} %copy-done), kind=kOutput, calls=%fused_computation.206 | convolution fusion | flops 1073741824 | bytes 18874368 | tf_op jit(solution)/shard_map/ikgd,jkd->kgij/dot_general | solution.py:35
  75.4 9.4 %fusion.12 = bf16[4,1,1024,1024]{2,3,0,1:T(8,128)(2,1)S(1)} fusion(f32[4,1024,1024]{2,1,0:T(8,128)} %fusion.168, bf16[1024,4,128]{2,0,1:T(8,128)(2,1)} %collective-permute-done.1, f32[4,1024]{1,0:T(4,128)S(1)} %copy.61, f32[4,1024]{1,0:T(4,128)S(1)} %copy-done.26, pred[1024,1024]{0,1:T(8,128)(4,1)S(1)} %copy-done.23, bf16[1024,4,128]{2,1,0:T(4,128)(2,1)S(1)} %copy-done.16), kind=kOutput, calls=%fused_computation.37 | convolution fusion | flops 1098907648 | bytes 28344320 | tf_op jit(solution)/shard_map/ikgd,jkd->kgij/dot_general | solution.py:38
  84.8 4.4 fusion.58
  89.2 5.3 bitcast_add_fusion.13
  94.8 12.6 %bitcast_add_fusion.6 = f32[1024,4,128]{2,0,1:T(8,128)} fusion(f32[1024,4,128]{2,0,1:T(8,128)} %collective-permute-done.22, f32[4,1024,1024]{2,1,0:T(8,128)} %fusion.168, f32[4,1024]{1,0:T(4,128)S(1)} %copy-done.26, pred[1024,1024]{0,1:T(8,128)(4,1)} %get-tuple-element.9, bf16[1024,4,128]{2,1,0:T(4,128)(2,1)} %param.10), kind=kOutput, calls=%fused_computation.118 | convolution fusion | flops 1091043328 | bytes 23085056 | tf_op jit(solution)/shard_map/kgij,ikgd->jkd/dot_general | solution.py:37
  107.4 8.1 %fusion.166 = f32[4,1024,1024]{2,1,0:T(8,128)} fusion(bf16[1024,4,128]{2,0,1:T(8,128)(2,1)S(1)} %collective-permute-done.2, bf16[1024,4,128]{2,1,0:T(4,128)(2,1)S(1)} %copy-done), kind=kOutput, calls=%fused_computation.204 | convolution fusion | flops 1073741824 | bytes 18874368 | tf_op jit(solution)/shard_map/ikgd,jkd->kgij/dot_general | solution.py:35
  115.6 11.6 %fusion.68 = f32[4,1024,128]{2,1,0:T(8,128)} fusion(f32[4,1024,1024]{2,1,0:T(8,128)} %fusion.166, f32[4,1024]{1,0:T(4,128)S(1)} %copy-done.26, pred[1024,1024]{0,1:T(8,128)(4,1)} %get-tuple-element.10, bf16[1024,4,128]{2,1,0:T(4,128)(2,1)} %param.10), kind=kOutput, calls=%fused_computation.98 | convolution fusion | flops 1090519040 | bytes 20987904 | tf_op jit(solution)/shard_map/kgij,ikgd->jkd/dot_general | solution.py:37
  129.2 9.4 %fusion.10 = bf16[4,1,1024,1024]{2,3,0,1:T(8,128)(2,1)S(1)} fusion(f32[4,1024,1024]{2,1,0:T(8,128)} %fusion.166, bf16[1024,4,128]{2,0,1:T(8,128)(2,1)} %collective-permute-done.3, f32[4,1024]{1,0:T(4,128)S(1)} %copy.61, f32[4,1024]{1,0:T(4,128)S(1)} %copy-done.26, pred[1024,1024]{0,1:T(8,128)(4,1)} %get-tuple-element.10, bf16[1024,4,128]{2,1,0:T(4,128)(2,1)} %param.10), kind=kOutput, calls=%fused_computation.31 | convolution fusion | flops 1098907648 | bytes 28344320 | tf_op jit(solution)/shard_map/ikgd,jkd->kgij/dot_general | solution.py:38
  138.6 3.6 fusion.52
  142.2 4.3 fusion.54
  146.5 26.0 %collective-permute-done.4 = bf16[1024,4,128]{2,0,1:T(8,128)(2,1)S(1)} collective-permute-done((bf16[1024,4,128]{2,0,1:T(8,128)(2,1)S(1)}, bf16[1024,4,128]{2,0,1:T(8,128)(2,1)S(1)}, u32[]{:S(2)}, u32[]{:S(2)}) %collective-permute-start.4) | collective-permute-done | bytes 1048608 | tf_op jit(solution)/shard_map/ppermute | solution.py:15
  172.6 8.1 %fusion.164 = f32[4,1024,1024]{2,1,0:T(8,128)} fusion(bf16[1024,4,128]{2,0,1:T(8,128)(2,1)S(1)} %collective-permute-done.4, bf16[1024,4,128]{2,1,0:T(4,128)(2,1)S(1)} %copy-done), kind=kOutput, calls=%fused_computation.202 | convolution fusion | flops 1073741824 | bytes 18874368 | tf_op jit(solution)/shard_map/ikgd,jkd->kgij/dot_general | solution.py:35
  180.7 3.1 collective-permute-done.5
  183.8 9.9 %fusion.8 = bf16[4,1,1024,1024]{2,3,0,1:T(8,128)(2,1)S(1)} fusion(f32[4,1024,1024]{2,1,0:T(8,128)} %fusion.164, bf16[1024,4,128]{2,0,1:T(8,128)(2,1)} %collective-permute-done.5, f32[4,1024]{1,0:T(4,128)S(1)} %copy.61, f32[4,1024]{1,0:T(4,128)S(1)} %copy-done.26, pred[1024,1024]{0,1:T(8,128)(4,1)S(1)} %copy-done.22, bf16[1024,4,128]{2,1,0:T(4,128)(2,1)S(1)} %copy-done.17), kind=kOutput, calls=%fused_computation.25 | convolution fusion | flops 1098907648 | bytes 28344320 | tf_op jit(solution)/shard_map/ikgd,jkd->kgij/dot_general | solution.py:38
  193.7 3.3 copy-done.4
  197.0 4.3 fusion.50
  201.3 11.6 %fusion.70 = f32[4,1024,128]{2,1,0:T(8,128)} fusion(f32[4,1024,1024]{2,1,0:T(8,128)} %fusion.164, f32[4,1024]{1,0:T(4,128)S(1)} %copy-done.26, pred[1024,1024]{0,1:T(8,128)(4,1)} %get-tuple-element.11, bf16[1024,4,128]{2,1,0:T(4,128)(2,1)} %param.10), kind=kOutput, calls=%fused_computation.99 | convolution fusion | flops 1090519040 | bytes 20987904 | tf_op jit(solution)/shard_map/kgij,ikgd->jkd/dot_general | solution.py:37
  212.8 7.2 %fusion.48 = f32[4,1024,128]{2,1,0:T(8,128)} fusion(bf16[4,1,1024,1024]{2,3,0,1:T(8,128)(2,1)} %copy-done.4, bf16[1024,4,128]{2,1,0:T(4,128)(2,1)S(1)} %copy-done), kind=kOutput, calls=%fused_computation.80 | convolution fusion | flops 1073741824 | bytes 11534336 | tf_op jit(solution)/shard_map/kgij,ikgd->jkd/dot_general | solution.py:41
  220.0 3.3 bitcast_add_fusion.12
  223.3 8.1 %fusion.162 = f32[4,1024,1024]{2,1,0:T(8,128)} fusion(bf16[1024,4,128]{2,0,1:T(8,128)(2,1)S(1)} %collective-permute-done.6, bf16[1024,4,128]{2,1,0:T(4,128)(2,1)S(1)} %copy-done), kind=kOutput, calls=%fused_computation.200 | convolution fusion | flops 1073741824 | bytes 18874368 | tf_op jit(solution)/shard_map/ikgd,jkd->kgij/dot_general | solution.py:35
  231.5 9.6 %fusion.6 = bf16[4,1,1024,1024]{2,3,0,1:T(8,128)(2,1)S(1)} fusion(f32[4,1024,1024]{2,1,0:T(8,128)} %fusion.162, bf16[1024,4,128]{2,0,1:T(8,128)(2,1)} %collective-permute-done.7, f32[4,1024]{1,0:T(4,128)S(1)} %copy.61, f32[4,1024]{1,0:T(4,128)S(1)} %copy-done.26, pred[1024,1024]{0,1:T(8,128)(4,1)S(1)} %copy-done.21, bf16[1024,4,128]{2,1,0:T(4,128)(2,1)S(1)} %copy-done.18), kind=kOutput, calls=%fused_computation.19 | convolution fusion | flops 1098907648 | bytes 28344320 | tf_op jit(solution)/shard_map/ikgd,jkd->kgij/dot_general | solution.py:38
  241.1 3.7 fusion.44
  244.8 3.1 bitcast_add_fusion.5
  249.5 4.3 fusion.46
  253.8 11.6 %fusion.72 = f32[4,1024,128]{2,1,0:T(8,128)} fusion(f32[4,1024,1024]{2,1,0:T(8,128)} %fusion.162, f32[4,1024]{1,0:T(4,128)S(1)} %copy-done.26, pred[1024,1024]{0,1:T(8,128)(4,1)} %get-tuple-element.12, bf16[1024,4,128]{2,1,0:T(4,128)(2,1)} %param.10), kind=kOutput, calls=%fused_computation.100 | convolution fusion | flops 1090519040 | bytes 20987904 | tf_op jit(solution)/shard_map/kgij,ikgd->jkd/dot_general | solution.py:37
  265.4 21.0 %collective-permute-done.8 = bf16[1024,4,128]{2,0,1:T(8,128)(2,1)S(1)} collective-permute-done((bf16[1024,4,128]{2,0,1:T(8,128)(2,1)S(1)}, bf16[1024,4,128]{2,0,1:T(8,128)(2,1)S(1)}, u32[]{:S(2)}, u32[]{:S(2)}) %collective-permute-start.8) | collective-permute-done | bytes 1048608 | tf_op jit(solution)/shard_map/ppermute | solution.py:15
  286.4 8.1 %fusion.160 = f32[4,1024,1024]{2,1,0:T(8,128)} fusion(bf16[1024,4,128]{2,0,1:T(8,128)(2,1)S(1)} %collective-permute-done.8, bf16[1024,4,128]{2,1,0:T(4,128)(2,1)S(1)} %copy-done), kind=kOutput, calls=%fused_computation.198 | convolution fusion | flops 1073741824 | bytes 18874368 | tf_op jit(solution)/shard_map/ikgd,jkd->kgij/dot_general | solution.py:35
  294.6 11.7 %fusion.74 = f32[4,1024,128]{2,1,0:T(8,128)} fusion(f32[4,1024,1024]{2,1,0:T(8,128)} %fusion.160, f32[4,1024]{1,0:T(4,128)S(1)} %copy-done.26, pred[1024,1024]{0,1:T(8,128)(4,1)} %get-tuple-element.13, bf16[1024,4,128]{2,1,0:T(4,128)(2,1)S(1)} %copy-done.19), kind=kOutput, calls=%fused_computation.101 | convolution fusion | flops 1090519040 | bytes 20987904 | tf_op jit(solution)/shard_map/kgij,ikgd->jkd/dot_general | solution.py:37
  306.3 9.6 %fusion.4 = bf16[4,1,1024,1024]{2,3,0,1:T(8,128)(2,1)S(1)} fusion(f32[4,1024,1024]{2,1,0:T(8,128)} %fusion.160, bf16[1024,4,128]{2,0,1:T(8,128)(2,1)} %collective-permute-done.9, f32[4,1024]{1,0:T(4,128)S(1)} %copy.61, f32[4,1024]{1,0:T(4,128)S(1)} %copy-done.26, pred[1024,1024]{0,1:T(8,128)(4,1)} %get-tuple-element.13, bf16[1024,4,128]{2,1,0:T(4,128)(2,1)} %param.10), kind=kOutput, calls=%fused_computation.13 | convolution fusion | flops 1098907648 | bytes 28344320 | tf_op jit(solution)/shard_map/ikgd,jkd->kgij/dot_general | solution.py:38
  317.8 4.3 fusion.42
  322.1 3.7 fusion.40
  325.8 3.2 bitcast_add_fusion.4
  329.2 8.1 %fusion.158 = f32[4,1024,1024]{2,1,0:T(8,128)} fusion(bf16[1024,4,128]{2,0,1:T(8,128)(2,1)S(1)} %collective-permute-done.10, bf16[1024,4,128]{2,1,0:T(4,128)(2,1)S(1)} %copy-done), kind=kOutput, calls=%fused_computation.196 | convolution fusion | flops 1073741824 | bytes 18874368 | tf_op jit(solution)/shard_map/ikgd,jkd->kgij/dot_general | solution.py:35
  337.3 18.7 %collective-permute-done.17 = f32[1024,4,128]{2,0,1:T(8,128)S(1)} collective-permute-done((f32[1024,4,128]{2,0,1:T(8,128)S(1)}, f32[1024,4,128]{2,0,1:T(8,128)S(1)}, u32[]{:S(2)}, u32[]{:S(2)}) %collective-permute-start.17) | collective-permute-done | bytes 2097184 | tf_op jit(solution)/shard_map/ppermute | solution.py:15
  357.6 11.7 %fusion.76 = f32[4,1024,128]{2,1,0:T(8,128)} fusion(f32[4,1024,1024]{2,1,0:T(8,128)} %fusion.158, f32[4,1024]{1,0:T(4,128)S(1)} %copy-done.26, pred[1024,1024]{0,1:T(8,128)(4,1)} %get-tuple-element.14, bf16[1024,4,128]{2,1,0:T(4,128)(2,1)} %param.10), kind=kOutput, calls=%fused_computation.102 | convolution fusion | flops 1090519040 | bytes 20987904 | tf_op jit(solution)/shard_map/kgij,ikgd->jkd/dot_general | solution.py:37
  369.2 9.2 %collective-permute-done.25 = f32[1024,4,128]{2,0,1:T(8,128)} collective-permute-done((f32[1024,4,128]{2,0,1:T(8,128)}, f32[1024,4,128]{2,0,1:T(8,128)}, u32[]{:S(2)}, u32[]{:S(2)}) %collective-permute-start.25) | collective-permute-done | bytes 2097184 | tf_op jit(solution)/shard_map/ppermute | solution.py:15
  378.4 3.8 bitcast_add_fusion.3
  382.2 9.5 %fusion.2 = bf16[4,1,1024,1024]{2,3,0,1:T(8,128)(2,1)S(1)} fusion(f32[4,1024,1024]{2,1,0:T(8,128)} %fusion.158, bf16[1024,4,128]{2,0,1:T(8,128)(2,1)} %collective-permute-done.11, f32[4,1024]{1,0:T(4,128)S(1)} %copy.61, f32[4,1024]{1,0:T(4,128)S(1)} %copy-done.26, pred[1024,1024]{0,1:T(8,128)(4,1)} %get-tuple-element.14, bf16[1024,4,128]{2,1,0:T(4,128)(2,1)S(1)} %copy-done.20), kind=kOutput, calls=%fused_computation.7 | convolution fusion | flops 1098907648 | bytes 28344320 | tf_op jit(solution)/shard_map/ikgd,jkd->kgij/dot_general | solution.py:38
  391.7 9.2 %collective-permute-done.18 = f32[1024,4,128]{2,0,1:T(8,128)} collective-permute-done((f32[1024,4,128]{2,0,1:T(8,128)}, f32[1024,4,128]{2,0,1:T(8,128)}, u32[]{:S(2)}, u32[]{:S(2)}) %collective-permute-start.18) | collective-permute-done | bytes 2097184 | tf_op jit(solution)/shard_map/ppermute | solution.py:15
  403.6 4.3 fusion.38
  410.2 35.6 %collective-permute-done.26 = f32[1024,4,128]{2,0,1:T(8,128)} collective-permute-done((f32[1024,4,128]{2,0,1:T(8,128)}, f32[1024,4,128]{2,0,1:T(8,128)}, u32[]{:S(2)}, u32[]{:S(2)}) %collective-permute-start.26) | collective-permute-done | bytes 2097184 | tf_op jit(solution)/shard_map/ppermute | solution.py:15
  445.9 3.2 bitcast_add_fusion.2
  449.1 8.1 %fusion.156 = f32[4,1024,1024]{2,1,0:T(8,128)} fusion(bf16[1024,4,128]{2,0,1:T(8,128)(2,1)S(1)} %collective-permute-done.12, bf16[1024,4,128]{2,1,0:T(4,128)(2,1)S(1)} %copy-done), kind=kOutput, calls=%fused_computation.194 | convolution fusion | flops 1073741824 | bytes 18874368 | tf_op jit(solution)/shard_map/ikgd,jkd->kgij/dot_general | solution.py:35
  457.2 11.1 %collective-permute-done.19 = f32[1024,4,128]{2,0,1:T(8,128)S(1)} collective-permute-done((f32[1024,4,128]{2,0,1:T(8,128)S(1)}, f32[1024,4,128]{2,0,1:T(8,128)S(1)}, u32[]{:S(2)}, u32[]{:S(2)}) %collective-permute-start.19) | collective-permute-done | bytes 2097184 | tf_op jit(solution)/shard_map/ppermute | solution.py:15
  469.6 9.6 %fusion = bf16[4,1,1024,1024]{2,3,0,1:T(8,128)(2,1)S(1)} fusion(f32[4,1024,1024]{2,1,0:T(8,128)} %fusion.156, bf16[1024,4,128]{2,0,1:T(8,128)(2,1)} %copy-done.25, f32[4,1024]{1,0:T(4,128)S(1)} %copy.61, f32[4,1024]{1,0:T(4,128)S(1)} %copy-done.26, pred[1024,1024]{0,1:T(8,128)(4,1)} %get-tuple-element.15, bf16[1024,4,128]{2,1,0:T(4,128)(2,1)} %param.10), kind=kOutput, calls=%fused_computation.1 | convolution fusion | flops 1098907648 | bytes 28344320 | tf_op jit(solution)/shard_map/ikgd,jkd->kgij/dot_general | solution.py:38
  479.2 11.6 %collective-permute-done.27 = f32[1024,4,128]{2,0,1:T(8,128)} collective-permute-done((f32[1024,4,128]{2,0,1:T(8,128)}, f32[1024,4,128]{2,0,1:T(8,128)}, u32[]{:S(2)}, u32[]{:S(2)}) %collective-permute-start.27) | collective-permute-done | bytes 2097184 | tf_op jit(solution)/shard_map/ppermute | solution.py:15
  490.8 3.1 bitcast_add_fusion.1
  496.5 16.8 %collective-permute-done.20 = f32[1024,4,128]{2,0,1:T(8,128)} collective-permute-done((f32[1024,4,128]{2,0,1:T(8,128)S(1)}, f32[1024,4,128]{2,0,1:T(8,128)}, u32[]{:S(2)}, u32[]{:S(2)}) %collective-permute-start.20) | collective-permute-done | bytes 2097184 | tf_op jit(solution)/shard_map/ppermute | solution.py:15
  513.3 3.2 bitcast_add_fusion.7
  516.4 11.8 %fusion.78 = f32[4,1024,128]{2,1,0:T(8,128)} fusion(f32[4,1024,1024]{2,1,0:T(8,128)} %fusion.156, f32[4,1024]{1,0:T(4,128)S(1)} %copy-done.26, pred[1024,1024]{0,1:T(8,128)(4,1)} %get-tuple-element.15, bf16[1024,4,128]{2,1,0:T(4,128)(2,1)} %param.10), kind=kOutput, calls=%fused_computation.103 | convolution fusion | flops 1090519040 | bytes 20987904 | tf_op jit(solution)/shard_map/kgij,ikgd->jkd/dot_general | solution.py:37
  528.2 7.6 %collective-permute-done.28 = f32[1024,4,128]{2,0,1:T(8,128)} collective-permute-done((f32[1024,4,128]{2,0,1:T(8,128)}, f32[1024,4,128]{2,0,1:T(8,128)}, u32[]{:S(2)}, u32[]{:S(2)}) %collective-permute-start.28) | collective-permute-done | bytes 2097184 | tf_op jit(solution)/shard_map/ppermute | solution.py:15
  535.7 3.4 bitcast_add_fusion
  539.5 11.3 %fusion.100 = bf16[1024,4,128]{2,0,1:T(8,128)(2,1)} fusion(bf16[1024,4,128]{2,0,1:T(8,128)(2,1)} %copy-done.6, bf16[4,1,1024,1024]{2,3,0,1:T(8,128)(2,1)} %copy-done.2, f32[4,1024,128]{2,1,0:T(8,128)} %fusion.38, f32[4,1024,128]{2,1,0:T(8,128)} %fusion.42, f32[4,1024,128]{2,1,0:T(8,128)} %fusion.46, f32[4,1024,128]{2,1,0:T(8,128)} %fusion.50, ...), kind=kOutput, calls=%fused_computation.139 | convolution fusion | flops 1078460416 | bytes 25165824 | tf_op jit(solution)/shard_map/kgij,jkd->ikgd/dot_general | solution.py:40
  550.8 3.0 copy.103
  553.8 15.7 %collective-permute-done.29 = bf16[1024,4,128]{2,0,1:T(8,128)(2,1)} collective-permute-done((bf16[1024,4,128]{2,0,1:T(8,128)(2,1)}, bf16[1024,4,128]{2,0,1:T(8,128)(2,1)}, u32[]{:S(2)}, u32[]{:S(2)}) %collective-permute-start.29) | collective-permute-done | bytes 1048608 | tf_op jit(solution)/shard_map/ppermute | solution.py:15
  569.4 3.0 copy.105
  (116 shorter events, 32.5 us)
Async XLA Ops:
  0.6 10.9 %copy-start = (bf16[1024,4,128]{2,1,0:T(4,128)(2,1)S(1)}, bf16[1024,4,128]{2,1,0:T(4,128)(2,1)}, u32[]{:S(2)}) copy-start(bf16[1024,4,128]{2,1,0:T(4,128)(2,1)} %param.6) | copy-start | bytes 3145732
  3.1 62.1 %collective-permute-start = (bf16[1024,4,128]{2,0,1:T(8,128)(2,1)}, bf16[1024,4,128]{2,0,1:T(8,128)(2,1)S(1)}, u32[]{:S(2)}, u32[]{:S(2)}) collective-permute-start(bf16[1024,4,128]{2,0,1:T(8,128)(2,1)} %copy.57), channel_id=1, source_target_pairs={{0,1},{1,2},{2,3},{3,4},{4,5},{5,6},{6,7},{7,0},{8,9},{9,10},{10,1... | collective-permute-start | bytes 3145736 | tf_op jit(solution)/shard_map/ppermute | solution.py:15
  5.9 67.5 %collective-permute-start.1 = (bf16[1024,4,128]{2,0,1:T(8,128)(2,1)}, bf16[1024,4,128]{2,0,1:T(8,128)(2,1)}, u32[]{:S(2)}, u32[]{:S(2)}) collective-permute-start(bf16[1024,4,128]{2,0,1:T(8,128)(2,1)} %copy.59), channel_id=1, source_target_pairs={{0,1},{1,2},{2,3},{3,4},{4,5},{5,6},{6,7},{7,0},{8,9},{9,10},{10,1... | collective-permute-start | bytes 3145736 | tf_op jit(solution)/shard_map/ppermute | solution.py:15
  20.9 6.5 %copy-start.14 = (bf16[1024,4,128]{2,1,0:T(4,128)(2,1)S(1)}, bf16[1024,4,128]{2,1,0:T(4,128)(2,1)}, u32[]{:S(2)}) copy-start(bf16[1024,4,128]{2,1,0:T(4,128)(2,1)} %param.8) | copy-start | bytes 3145732
  20.9 6.5 %copy-start.26 = (f32[4,1024]{1,0:T(4,128)S(1)}, f32[4,1024]{1,0:T(4,128)}, u32[]{:S(2)}) copy-start(f32[4,1024]{1,0:T(4,128)} %param.11) | copy-start | bytes 49156
  20.9 6.5 %copy-start.15 = (bf16[1024,4,128]{2,1,0:T(4,128)(2,1)S(1)}, bf16[1024,4,128]{2,1,0:T(4,128)(2,1)}, u32[]{:S(2)}) copy-start(bf16[1024,4,128]{2,1,0:T(4,128)(2,1)} %param.10) | copy-start | bytes 3145732
  27.4 9.6 %copy-start.24 = (pred[1024,1024]{0,1:T(8,128)(4,1)}, pred[1024,1024]{0,1:T(8,128)(4,1)S(1)}, u32[]{:S(2)}) copy-start(pred[1024,1024]{0,1:T(8,128)(4,1)S(1)} %get-tuple-element.16) | copy-start | bytes 3145732
  37.0 3.3 copy-start.3
  44.0 13.5 %copy-start.1 = (bf16[1024,4,128]{2,1,0:T(4,128)(2,1)S(1)}, bf16[1024,4,128]{2,1,0:T(4,128)(2,1)}, u32[]{:S(2)}) copy-start(bf16[1024,4,128]{2,1,0:T(4,128)(2,1)} %param.7) | copy-start | bytes 3145732
  44.0 45.2 %collective-permute-start.14 = (f32[1024,4,128]{2,0,1:T(8,128)}, f32[1024,4,128]{2,0,1:T(8,128)}, u32[]{:S(2)}, u32[]{:S(2)}) collective-permute-start(f32[1024,4,128]{2,0,1:T(8,128)} %fusion.93), channel_id=1, source_target_pairs={{0,1},{1,2},{2,3},{3,4},{4,5},{5,6},{6,7},{7,0},{8,9},{9,10},{10,1... | collective-permute-start | bytes 6291464 | tf_op jit(solution)/shard_map/ppermute | solution.py:15
  55.9 38.9 %collective-permute-start.22 = (f32[1024,4,128]{2,0,1:T(8,128)}, f32[1024,4,128]{2,0,1:T(8,128)}, u32[]{:S(2)}, u32[]{:S(2)}) collective-permute-start(f32[1024,4,128]{2,0,1:T(8,128)} %fusion.90), channel_id=1, source_target_pairs={{0,1},{1,2},{2,3},{3,4},{4,5},{5,6},{6,7},{7,0},{8,9},{9,10},{10,1... | collective-permute-start | bytes 6291464 | tf_op jit(solution)/shard_map/ppermute | solution.py:15
  65.1 10.3 %copy-start.16 = (bf16[1024,4,128]{2,1,0:T(4,128)(2,1)S(1)}, bf16[1024,4,128]{2,1,0:T(4,128)(2,1)}, u32[]{:S(2)}) copy-start(bf16[1024,4,128]{2,1,0:T(4,128)(2,1)} %param.10) | copy-start | bytes 3145732
  65.1 10.3 %copy-start.23 = (pred[1024,1024]{0,1:T(8,128)(4,1)S(1)}, pred[1024,1024]{0,1:T(8,128)(4,1)}, u32[]{:S(2)}) copy-start(pred[1024,1024]{0,1:T(8,128)(4,1)} %get-tuple-element.9) | copy-start | bytes 3145732
  65.1 42.3 %collective-permute-start.2 = (bf16[1024,4,128]{2,0,1:T(8,128)(2,1)S(1)}, bf16[1024,4,128]{2,0,1:T(8,128)(2,1)S(1)}, u32[]{:S(2)}, u32[]{:S(2)}) collective-permute-start(bf16[1024,4,128]{2,0,1:T(8,128)(2,1)S(1)} %collective-permute-done), channel_id=1, source_target_pairs={{0,1},{1,2},{2,3},{3,4},{4,5},{5,6},{6,7},{7,0},{8,9},{9,10},{10,1... | collective-permute-start | bytes 3145736 | tf_op jit(solution)/shard_map/ppermute | solution.py:15
  73.4 53.7 %collective-permute-start.3 = (bf16[1024,4,128]{2,0,1:T(8,128)(2,1)}, bf16[1024,4,128]{2,0,1:T(8,128)(2,1)}, u32[]{:S(2)}, u32[]{:S(2)}) collective-permute-start(bf16[1024,4,128]{2,0,1:T(8,128)(2,1)} %collective-permute-done.1), channel_id=1, source_target_pairs={{0,1},{1,2},{2,3},{3,4},{4,5},{5,6},{6,7},{7,0},{8,9},{9,10},{10,1... | collective-permute-start | bytes 3145736 | tf_op jit(solution)/shard_map/ppermute | solution.py:15
  94.5 125.5 %collective-permute-start.15 = (f32[1024,4,128]{2,0,1:T(8,128)}, f32[1024,4,128]{2,0,1:T(8,128)}, u32[]{:S(2)}, u32[]{:S(2)}) collective-permute-start(f32[1024,4,128]{2,0,1:T(8,128)} %bitcast_add_fusion.13), channel_id=1, source_target_pairs={{0,1},{1,2},{2,3},{3,4},{4,5},{5,6},{6,7},{7,0},{8,9},{9,10},{10,1... | collective-permute-start | bytes 6291464 | tf_op jit(solution)/shard_map/ppermute | solution.py:15
  107.3 137.5 %collective-permute-start.23 = (f32[1024,4,128]{2,0,1:T(8,128)}, f32[1024,4,128]{2,0,1:T(8,128)}, u32[]{:S(2)}, u32[]{:S(2)}) collective-permute-start(f32[1024,4,128]{2,0,1:T(8,128)} %bitcast_add_fusion.6), channel_id=1, source_target_pairs={{0,1},{1,2},{2,3},{3,4},{4,5},{5,6},{6,7},{7,0},{8,9},{9,10},{10,1... | collective-permute-start | bytes 6291464 | tf_op jit(solution)/shard_map/ppermute | solution.py:15
  107.4 65.2 %collective-permute-start.4 = (bf16[1024,4,128]{2,0,1:T(8,128)(2,1)S(1)}, bf16[1024,4,128]{2,0,1:T(8,128)(2,1)S(1)}, u32[]{:S(2)}, u32[]{:S(2)}) collective-permute-start(bf16[1024,4,128]{2,0,1:T(8,128)(2,1)S(1)} %collective-permute-done.2), channel_id=1, source_target_pairs={{0,1},{1,2},{2,3},{3,4},{4,5},{5,6},{6,7},{7,0},{8,9},{9,10},{10,1... | collective-permute-start | bytes 3145736 | tf_op jit(solution)/shard_map/ppermute | solution.py:15
  127.1 56.6 %collective-permute-start.5 = (bf16[1024,4,128]{2,0,1:T(8,128)(2,1)}, bf16[1024,4,128]{2,0,1:T(8,128)(2,1)}, u32[]{:S(2)}, u32[]{:S(2)}) collective-permute-start(bf16[1024,4,128]{2,0,1:T(8,128)(2,1)} %collective-permute-done.3), channel_id=1, source_target_pairs={{0,1},{1,2},{2,3},{3,4},{4,5},{5,6},{6,7},{7,0},{8,9},{9,10},{10,1... | collective-permute-start | bytes 3145736 | tf_op jit(solution)/shard_map/ppermute | solution.py:15
  146.5 37.3 %copy-start.17 = (bf16[1024,4,128]{2,1,0:T(4,128)(2,1)S(1)}, bf16[1024,4,128]{2,1,0:T(4,128)(2,1)}, u32[]{:S(2)}) copy-start(bf16[1024,4,128]{2,1,0:T(4,128)(2,1)} %param.10) | copy-start | bytes 3145732
  146.5 37.3 %copy-start.22 = (pred[1024,1024]{0,1:T(8,128)(4,1)S(1)}, pred[1024,1024]{0,1:T(8,128)(4,1)}, u32[]{:S(2)}) copy-start(pred[1024,1024]{0,1:T(8,128)(4,1)} %get-tuple-element.11) | copy-start | bytes 3145732
  172.5 50.8 %collective-permute-start.6 = (bf16[1024,4,128]{2,0,1:T(8,128)(2,1)S(1)}, bf16[1024,4,128]{2,0,1:T(8,128)(2,1)S(1)}, u32[]{:S(2)}, u32[]{:S(2)}) collective-permute-start(bf16[1024,4,128]{2,0,1:T(8,128)(2,1)S(1)} %collective-permute-done.4), channel_id=1, source_target_pairs={{0,1},{1,2},{2,3},{3,4},{4,5},{5,6},{6,7},{7,0},{8,9},{9,10},{10,1... | collective-permute-start | bytes 3145736 | tf_op jit(solution)/shard_map/ppermute | solution.py:15
  183.8 47.7 %collective-permute-start.7 = (bf16[1024,4,128]{2,0,1:T(8,128)(2,1)}, bf16[1024,4,128]{2,0,1:T(8,128)(2,1)}, u32[]{:S(2)}, u32[]{:S(2)}) collective-permute-start(bf16[1024,4,128]{2,0,1:T(8,128)(2,1)} %collective-permute-done.5), channel_id=1, source_target_pairs={{0,1},{1,2},{2,3},{3,4},{4,5},{5,6},{6,7},{7,0},{8,9},{9,10},{10,1... | collective-permute-start | bytes 3145736 | tf_op jit(solution)/shard_map/ppermute | solution.py:15
  193.7 3.3 copy-start.4
  212.8 7.2 %copy-start.13 = (f32[4,1024,128]{2,1,0:T(8,128)S(1)}, f32[4,1024,128]{2,1,0:T(8,128)}, u32[]{:S(2)}) copy-start(f32[4,1024,128]{2,1,0:T(8,128)} %fusion.52) | copy-start | bytes 6291460
  223.3 8.2 %copy-start.18 = (bf16[1024,4,128]{2,1,0:T(4,128)(2,1)S(1)}, bf16[1024,4,128]{2,1,0:T(4,128)(2,1)}, u32[]{:S(2)}) copy-start(bf16[1024,4,128]{2,1,0:T(4,128)(2,1)} %param.10) | copy-start | bytes 3145732
  223.3 8.2 %copy-start.21 = (pred[1024,1024]{0,1:T(8,128)(4,1)S(1)}, pred[1024,1024]{0,1:T(8,128)(4,1)}, u32[]{:S(2)}) copy-start(pred[1024,1024]{0,1:T(8,128)(4,1)} %get-tuple-element.12) | copy-start | bytes 3145732
  223.3 92.6 %collective-permute-start.16 = (f32[1024,4,128]{2,0,1:T(8,128)}, f32[1024,4,128]{2,0,1:T(8,128)}, u32[]{:S(2)}, u32[]{:S(2)}) collective-permute-start(f32[1024,4,128]{2,0,1:T(8,128)} %bitcast_add_fusion.12), channel_id=1, source_target_pairs={{0,1},{1,2},{2,3},{3,4},{4,5},{5,6},{6,7},{7,0},{8,9},{9,10},{10,1... | collective-permute-start | bytes 6291464 | tf_op jit(solution)/shard_map/ppermute | solution.py:15
  241.1 3.7 copy-start.12
  247.9 77.9 %collective-permute-start.24 = (f32[1024,4,128]{2,0,1:T(8,128)}, f32[1024,4,128]{2,0,1:T(8,128)}, u32[]{:S(2)}, u32[]{:S(2)}) collective-permute-start(f32[1024,4,128]{2,0,1:T(8,128)} %bitcast_add_fusion.5), channel_id=1, source_target_pairs={{0,1},{1,2},{2,3},{3,4},{4,5},{5,6},{6,7},{7,0},{8,9},{9,10},{10,1... | collective-permute-start | bytes 6291464 | tf_op jit(solution)/shard_map/ppermute | solution.py:15
  247.9 38.5 %collective-permute-start.8 = (bf16[1024,4,128]{2,0,1:T(8,128)(2,1)S(1)}, bf16[1024,4,128]{2,0,1:T(8,128)(2,1)S(1)}, u32[]{:S(2)}, u32[]{:S(2)}) collective-permute-start(bf16[1024,4,128]{2,0,1:T(8,128)(2,1)S(1)} %collective-permute-done.6), channel_id=1, source_target_pairs={{0,1},{1,2},{2,3},{3,4},{4,5},{5,6},{6,7},{7,0},{8,9},{9,10},{10,1... | collective-permute-start | bytes 3145736 | tf_op jit(solution)/shard_map/ppermute | solution.py:15
  249.5 56.8 %collective-permute-start.9 = (bf16[1024,4,128]{2,0,1:T(8,128)(2,1)}, bf16[1024,4,128]{2,0,1:T(8,128)(2,1)}, u32[]{:S(2)}, u32[]{:S(2)}) collective-permute-start(bf16[1024,4,128]{2,0,1:T(8,128)(2,1)} %collective-permute-done.7), channel_id=1, source_target_pairs={{0,1},{1,2},{2,3},{3,4},{4,5},{5,6},{6,7},{7,0},{8,9},{9,10},{10,1... | collective-permute-start | bytes 3145736 | tf_op jit(solution)/shard_map/ppermute | solution.py:15
  286.4 8.1 %copy-start.19 = (bf16[1024,4,128]{2,1,0:T(4,128)(2,1)S(1)}, bf16[1024,4,128]{2,1,0:T(4,128)(2,1)}, u32[]{:S(2)}) copy-start(bf16[1024,4,128]{2,1,0:T(4,128)(2,1)} %param.10) | copy-start | bytes 3145732
  306.2 9.7 %copy-start.11 = (f32[4,1024,128]{2,1,0:T(8,128)S(1)}, f32[4,1024,128]{2,1,0:T(8,128)}, u32[]{:S(2)}) copy-start(f32[4,1024,128]{2,1,0:T(8,128)} %fusion.48) | copy-start | bytes 6291460
  306.2 22.9 %collective-permute-start.10 = (bf16[1024,4,128]{2,0,1:T(8,128)(2,1)S(1)}, bf16[1024,4,128]{2,0,1:T(8,128)(2,1)S(1)}, u32[]{:S(2)}, u32[]{:S(2)}) collective-permute-start(bf16[1024,4,128]{2,0,1:T(8,128)(2,1)S(1)} %collective-permute-done.8), channel_id=1, source_target_pairs={{0,1},{1,2},{2,3},{3,4},{4,5},{5,6},{6,7},{7,0},{8,9},{9,10},{10,1... | collective-permute-start | bytes 3145736 | tf_op jit(solution)/shard_map/ppermute | solution.py:15
  306.2 63.0 %collective-permute-start.11 = (bf16[1024,4,128]{2,0,1:T(8,128)(2,1)}, bf16[1024,4,128]{2,0,1:T(8,128)(2,1)}, u32[]{:S(2)}, u32[]{:S(2)}) collective-permute-start(bf16[1024,4,128]{2,0,1:T(8,128)(2,1)} %collective-permute-done.9), channel_id=1, source_target_pairs={{0,1},{1,2},{2,3},{3,4},{4,5},{5,6},{6,7},{7,0},{8,9},{9,10},{10,1... | collective-permute-start | bytes 3145736 | tf_op jit(solution)/shard_map/ppermute | solution.py:15
  317.7 38.2 %collective-permute-start.17 = (f32[1024,4,128]{2,0,1:T(8,128)S(1)}, f32[1024,4,128]{2,0,1:T(8,128)S(1)}, u32[]{:S(2)}, u32[]{:S(2)}) collective-permute-start(f32[1024,4,128]{2,0,1:T(8,128)S(1)} %bitcast_add_fusion.11), channel_id=1, source_target_pairs={{0,1},{1,2},{2,3},{3,4},{4,5},{5,6},{6,7},{7,0},{8,9},{9,10},{10,1... | collective-permute-start | bytes 6291464 | tf_op jit(solution)/shard_map/ppermute | solution.py:15
  322.1 3.7 copy-start.8
  329.0 27.0 %copy-start.9 = (f32[4,1024,128]{2,1,0:T(8,128)S(1)}, f32[4,1024,128]{2,1,0:T(8,128)}, u32[]{:S(2)}) copy-start(f32[4,1024,128]{2,1,0:T(8,128)} %fusion.44) | copy-start | bytes 6291460
  329.0 49.5 %collective-permute-start.25 = (f32[1024,4,128]{2,0,1:T(8,128)}, f32[1024,4,128]{2,0,1:T(8,128)}, u32[]{:S(2)}, u32[]{:S(2)}) collective-permute-start(f32[1024,4,128]{2,0,1:T(8,128)} %bitcast_add_fusion.4), channel_id=1, source_target_pairs={{0,1},{1,2},{2,3},{3,4},{4,5},{5,6},{6,7},{7,0},{8,9},{9,10},{10,1... | collective-permute-start | bytes 6291464 | tf_op jit(solution)/shard_map/ppermute | solution.py:15
  357.5 43.4 %collective-permute-start.18 = (f32[1024,4,128]{2,0,1:T(8,128)}, f32[1024,4,128]{2,0,1:T(8,128)}, u32[]{:S(2)}, u32[]{:S(2)}) collective-permute-start(f32[1024,4,128]{2,0,1:T(8,128)} %bitcast_add_fusion.10), channel_id=1, source_target_pairs={{0,1},{1,2},{2,3},{3,4},{4,5},{5,6},{6,7},{7,0},{8,9},{9,10},{10,1... | collective-permute-start | bytes 6291464 | tf_op jit(solution)/shard_map/ppermute | solution.py:15
  357.6 24.7 %copy-start.20 = (bf16[1024,4,128]{2,1,0:T(4,128)(2,1)S(1)}, bf16[1024,4,128]{2,1,0:T(4,128)(2,1)}, u32[]{:S(2)}) copy-start(bf16[1024,4,128]{2,1,0:T(4,128)(2,1)} %param.10) | copy-start | bytes 3145732
  369.2 79.9 %collective-permute-start.12 = (bf16[1024,4,128]{2,0,1:T(8,128)(2,1)S(1)}, bf16[1024,4,128]{2,0,1:T(8,128)(2,1)S(1)}, u32[]{:S(2)}, u32[]{:S(2)}) collective-permute-start(bf16[1024,4,128]{2,0,1:T(8,128)(2,1)S(1)} %collective-permute-done.10), channel_id=1, source_target_pairs={{0,1},{1,2},{2,3},{3,4},{4,5},{5,6},{6,7},{7,0},{8,9},{9,10},{10,1... | collective-permute-start | bytes 3145736 | tf_op jit(solution)/shard_map/ppermute | solution.py:15
  369.2 99.4 %collective-permute-start.13 = (bf16[1024,4,128]{2,0,1:T(8,128)(2,1)}, bf16[1024,4,128]{2,0,1:T(8,128)(2,1)S(1)}, u32[]{:S(2)}, u32[]{:S(2)}) collective-permute-start(bf16[1024,4,128]{2,0,1:T(8,128)(2,1)} %collective-permute-done.11), channel_id=1, source_target_pairs={{0,1},{1,2},{2,3},{3,4},{4,5},{5,6},{6,7},{7,0},{8,9},{9,10},{10,1... | collective-permute-start | bytes 3145736 | tf_op jit(solution)/shard_map/ppermute | solution.py:15
  382.2 63.6 %collective-permute-start.26 = (f32[1024,4,128]{2,0,1:T(8,128)}, f32[1024,4,128]{2,0,1:T(8,128)}, u32[]{:S(2)}, u32[]{:S(2)}) collective-permute-start(f32[1024,4,128]{2,0,1:T(8,128)} %bitcast_add_fusion.3), channel_id=1, source_target_pairs={{0,1},{1,2},{2,3},{3,4},{4,5},{5,6},{6,7},{7,0},{8,9},{9,10},{10,1... | collective-permute-start | bytes 6291464 | tf_op jit(solution)/shard_map/ppermute | solution.py:15
  403.3 65.0 %collective-permute-start.19 = (f32[1024,4,128]{2,0,1:T(8,128)S(1)}, f32[1024,4,128]{2,0,1:T(8,128)S(1)}, u32[]{:S(2)}, u32[]{:S(2)}) collective-permute-start(f32[1024,4,128]{2,0,1:T(8,128)S(1)} %bitcast_add_fusion.9), channel_id=1, source_target_pairs={{0,1},{1,2},{2,3},{3,4},{4,5},{5,6},{6,7},{7,0},{8,9},{9,10},{10,1... | collective-permute-start | bytes 6291464 | tf_op jit(solution)/shard_map/ppermute | solution.py:15
  407.9 37.9 %copy-start.7 = (f32[4,1024,128]{2,1,0:T(8,128)S(1)}, f32[4,1024,128]{2,1,0:T(8,128)}, u32[]{:S(2)}) copy-start(f32[4,1024,128]{2,1,0:T(8,128)} %fusion.74) | copy-start | bytes 6291460
  449.1 41.7 %collective-permute-start.27 = (f32[1024,4,128]{2,0,1:T(8,128)}, f32[1024,4,128]{2,0,1:T(8,128)}, u32[]{:S(2)}, u32[]{:S(2)}) collective-permute-start(f32[1024,4,128]{2,0,1:T(8,128)} %bitcast_add_fusion.2), channel_id=1, source_target_pairs={{0,1},{1,2},{2,3},{3,4},{4,5},{5,6},{6,7},{7,0},{8,9},{9,10},{10,1... | collective-permute-start | bytes 6291464 | tf_op jit(solution)/shard_map/ppermute | solution.py:15
  449.1 8.2 %copy-start.6 = (bf16[1024,4,128]{2,0,1:T(8,128)(2,1)}, bf16[1024,4,128]{2,0,1:T(8,128)(2,1)S(1)}, u32[]{:S(2)}) copy-start(bf16[1024,4,128]{2,0,1:T(8,128)(2,1)S(1)} %collective-permute-done.12) | copy-start | bytes 3145732
  468.5 44.7 %collective-permute-start.20 = (f32[1024,4,128]{2,0,1:T(8,128)S(1)}, f32[1024,4,128]{2,0,1:T(8,128)}, u32[]{:S(2)}, u32[]{:S(2)}) collective-permute-start(f32[1024,4,128]{2,0,1:T(8,128)S(1)} %bitcast_add_fusion.8), channel_id=1, source_target_pairs={{0,1},{1,2},{2,3},{3,4},{4,5},{5,6},{6,7},{7,0},{8,9},{9,10},{10,1... | collective-permute-start | bytes 6291464 | tf_op jit(solution)/shard_map/ppermute | solution.py:15
  468.6 1.0 copy-start.25
  469.6 21.2 %copy-start.10 = (f32[4,1024,128]{2,1,0:T(8,128)S(1)}, f32[4,1024,128]{2,1,0:T(8,128)}, u32[]{:S(2)}) copy-start(f32[4,1024,128]{2,1,0:T(8,128)} %fusion.76) | copy-start | bytes 6291460
  479.2 17.3 %copy-start.2 = (bf16[4,1,1024,1024]{2,3,0,1:T(8,128)(2,1)}, bf16[4,1,1024,1024]{2,3,0,1:T(8,128)(2,1)S(1)}, u32[]{:S(2)}) copy-start(bf16[4,1,1024,1024]{2,3,0,1:T(8,128)(2,1)S(1)} %fusion) | copy-start | bytes 25165828
  493.9 41.8 %collective-permute-start.28 = (f32[1024,4,128]{2,0,1:T(8,128)}, f32[1024,4,128]{2,0,1:T(8,128)}, u32[]{:S(2)}, u32[]{:S(2)}) collective-permute-start(f32[1024,4,128]{2,0,1:T(8,128)} %bitcast_add_fusion.1), channel_id=1, source_target_pairs={{0,1},{1,2},{2,3},{3,4},{4,5},{5,6},{6,7},{7,0},{8,9},{9,10},{10,1... | collective-permute-start | bytes 6291464 | tf_op jit(solution)/shard_map/ppermute | solution.py:15
  516.4 23.0 %copy-start.5 = (f32[4,1024,128]{2,1,0:T(8,128)S(1)}, f32[4,1024,128]{2,1,0:T(8,128)}, u32[]{:S(2)}) copy-start(f32[4,1024,128]{2,1,0:T(8,128)} %fusion.62) | copy-start | bytes 6291460
  516.4 56.0 %collective-permute-start.21 = (f32[1024,4,128]{2,0,1:T(8,128)}, f32[1024,4,128]{2,0,1:T(8,128)}, u32[]{:S(2)}, u32[]{:S(2)}) collective-permute-start(f32[1024,4,128]{2,0,1:T(8,128)} %bitcast_add_fusion.7), channel_id=1, source_target_pairs={{0,1},{1,2},{2,3},{3,4},{4,5},{5,6},{6,7},{7,0},{8,9},{9,10},{10,1... | collective-permute-start | bytes 6291464 | tf_op jit(solution)/shard_map/ppermute | solution.py:15
  539.2 30.3 %collective-permute-start.29 = (bf16[1024,4,128]{2,0,1:T(8,128)(2,1)}, bf16[1024,4,128]{2,0,1:T(8,128)(2,1)}, u32[]{:S(2)}, u32[]{:S(2)}) collective-permute-start(bf16[1024,4,128]{2,0,1:T(8,128)(2,1)} %bitcast_add_fusion), channel_id=1, source_target_pairs={{0,1},{1,2},{2,3},{3,4},{4,5},{5,6},{6,7},{7,0},{8,9},{9,10},{10,1... | collective-permute-start | bytes 3145736 | tf_op jit(solution)/shard_map/ppermute | solution.py:15
where the time goes:
time: 585 us; the launch traced here: 577 us
  matrix products  314 us (54%)
  waiting for transfers between devices  186 us (32%)
  other arithmetic  43.3 us (7%)
  local copies, waits for them, and re-layouts  20.4 us (3%)
  starting transfers between devices  12.2 us (2%)
    ppermute x30, waiting for transfers between devices, shift(): return lax.ppermute(x, 'cp', perm)  186 us
    dot_general x8, matrix products, local(): jnp.einsum('kgij,ikgd->jkd', pr.astype(bf16), dos, preferred_element_type...  94.1 us
    dot_general x8, matrix products, local(): dp = jnp.einsum('ikgd,jkd->kgij', dos, v, preferred_element_type=f32)  76.6 us
    dot_general x8, matrix products, local(): s = jnp.einsum('ikgd,jkd->kgij', qs, k, preferred_element_type=f32) * scale  66.4 us
    dot_general x8, matrix products, local(): dq = dq + jnp.einsum('kgij,jkd->ikgd', ds, k, preferred_element_type=f32)  44.7 us
    dot_general x8, matrix products, local(): dk = dk + jnp.einsum('kgij,ikgd->jkd', ds, qs, preferred_element_type=f32)  31.8 us
    unnamed x59, local copies, waits for them, and re-layouts  20.2 us
    add x6, other arithmetic, local(): dv + jnp.einsum('kgij,ikgd->jkd', pr.astype(bf16), dos, preferred_element...  19.8 us
  transfers between devices with their start and end apart: 30, of which 12 were waited for; matrix products, arithmetic and copies ran while one was open for 63% of the time, Pallas kernels for 0%

commit v1 on v0

v1 whole, which is shorter than its diff:
```python
import functools
import math

import jax
import jax.numpy as jnp
from jax import lax
from jax.experimental import pallas as pl
from jax.experimental.pallas import tpu as pltpu
from jax.sharding import PartitionSpec as P

F32, BF16 = jnp.float32, jnp.bfloat16
D = 128
R = 128
MESH = pl.DeviceIdType.MESH
NT = (((1,), (1,)), ((), ()))
NN = (((1,), (0,)), ((), ()))


def dot(a, b, dims=NN):
    return lax.dot_general(a, b, dims, preferred_element_type=F32)


def deinterleave(rows, heads):
    r = lax.broadcasted_iota(jnp.int32, (rows, rows), 0)
    c = lax.broadcasted_iota(jnp.int32, (rows, rows), 1)
    m = rows // heads
    return jnp.where(c == (r % m) * heads + r // m, 1.0, 0.0).astype(BF16)


def interleave(rows, heads):
    r = lax.broadcasted_iota(jnp.int32, (rows, rows), 0)
    c = lax.broadcasted_iota(jnp.int32, (rows, rows), 1)
    m = rows // heads
    return jnp.where(r == (c % m) * heads + c // m, 1.0, 0.0).astype(BF16)


def exchange_kernel(nc, q_h, do_h, k_h, v_h, o_h, lse_h, okv, oq,
                    q_r, do_r, k_r, v_r, o_r, lse_r, perm, orel,
                    sb, sbs, G, Gs, H, Hs, kt, dk_acc, dv_acc, dqo, dqp, X, skv, sq,
                    lsem, ds, dr, ss, sr, fs, fr, gs, gr, ks, kr, qs, qr, xs, xr):
    me = lax.axis_index('cp')
    z, c = me // 2, me % 2
    scale = D ** -0.5
    log2e = math.log2(math.e)
    partner = {'cp': z * 2 + (1 - c)}
    others = [lax.rem(z + i, 4) for i in (1, 2, 3)]
    home = [{'cp': zz * 2 + c} for zz in others]

    loads = [pltpu.make_async_copy(s, d, lsem.at[i]) for i, (s, d) in enumerate(
        ((q_h, q_r), (do_h, do_r), (k_h, k_r), (v_h, v_r), (o_h, o_r), (lse_h, lse_r)))]
    for x in loads:
        x.start()

    barrier = pltpu.get_barrier_semaphore()
    for dev in home + [partner]:
        pl.semaphore_signal(barrier, inc=1, device_id=dev, device_id_type=MESH)
    perm[...] = deinterleave(256, 4)
    for x in loads:
        x.wait()
    pl.semaphore_wait(barrier, 4)

    def remote(src, dst, ssem, rsem, dev):
        return pltpu.make_async_remote_copy(src_ref=src, dst_ref=dst, send_sem=ssem, recv_sem=rsem,
                                            device_id=dev, device_id_type=MESH)

    def data(a, i):
        return remote(sb.at[others[i], a], G.at[a, z], ds.at[a, others[i]], dr.at[a, z], home[i])

    def stat(a, i):
        return remote(sbs.at[others[i], a], Gs.at[a, z], ss.at[a, others[i]], sr.at[a, z], home[i])

    def data_in(a, i):
        return remote(sb.at[others[i], a], G.at[a, others[i]], ds.at[a, others[i]], dr.at[a, others[i]], home[i])

    def stat_in(a, i):
        return remote(sbs.at[others[i], a], Gs.at[a, others[i]], ss.at[a, others[i]], sr.at[a, others[i]], home[i])

    def fwd(a, zz):
        return remote(G.at[a, zz, pl.ds(0, 2)], H.at[a, zz], fs.at[a, zz], fr.at[a, zz], partner)

    def fwd_stat(a, zz):
        return remote(Gs.at[a, zz], Hs.at[a, zz], gs.at[a, zz], gr.at[a, zz], partner)

    def kv_out(a, i):
        return remote(skv.at[a, others[i]], okv.at[z, a], ks.at[a, others[i]], kr.at[a, z], home[i])

    def kv_in(a, i):
        return remote(skv.at[a, others[i]], okv.at[others[i], a], ks.at[a, others[i]], kr.at[a, others[i]], home[i])

    def kv_own(a):
        return pltpu.make_async_copy(skv.at[a, z], okv.at[z, a], ks.at[a, z])

    def q_out(a, i):
        return remote(sq.at[a, others[i]], oq.at[z, a], qs.at[a, others[i]], qr.at[a, z], home[i])

    def q_in(a, i):
        return remote(sq.at[a, others[i]], oq.at[others[i], a], qs.at[a, others[i]], qr.at[a, others[i]], home[i])

    def q_own(a):
        return pltpu.make_async_copy(sq.at[a, z], oq.at[z, a], qs.at[a, z])

    def cross(a):
        return remote(dqp.at[a], X.at[a], xs.at[a], xr.at[a], partner)

    @pl.loop(0, nc)
    def _(step):
        a = nc - 1 - step
        pm = perm[...]
        for b in range(2):
            rows = pl.ds(pl.multiple_of(a * 512 + b * 256, 256), 256)
            for t, ref in enumerate((q_r, do_r, k_r, v_r)):
                y = dot(pm, ref[rows, :]).astype(BF16)
                for h in range(4):
                    sb[h, a, t, b * 64:(b + 1) * 64, :] = y[h * 64:(h + 1) * 64]
            y = dot(pm, o_r[rows, :]).astype(BF16)
            for h in range(4):
                orel[h, b * 64:(b + 1) * 64, :] = y[h * 64:(h + 1) * 64]
        eye = (lax.broadcasted_iota(jnp.int32, (R, R), 0)
               == lax.broadcasted_iota(jnp.int32, (R, R), 1))
        for h in range(4):
            prod = dot(sb[h, a, 1], orel[h], NT)
            delta = jnp.sum(jnp.where(eye, prod, 0.0), axis=0, keepdims=True)
            sbs[h, a, 0:1, :] = lse_r[h:h + 1, pl.ds(pl.multiple_of(a * R, R), R)] * log2e
            sbs[h, a, 1:2, :] = delta
        G[a, z] = sb[z, a]
        Gs[a, z] = sbs[z, a]
        for i in range(3):
            data(a, i).start()
        for i in range(3):
            stat(a, i).start()
        fwd(a, z).start()
        fwd_stat(a, z).start()

    def tile(a, b, j, diagonal):
        src, stats, dq = (G, Gs, dqo) if j < 2 else (H, Hs, dqp)
        jj = j % 2
        kk = G[a, :, 2].reshape(4 * R, D)
        vv = G[a, :, 3].reshape(4 * R, D)
        qq = src[b, 2 * jj:2 * jj + 2, 0].reshape(2 * R, D)
        dd = src[b, 2 * jj:2 * jj + 2, 1].reshape(2 * R, D)
        row = [jnp.concatenate([stats[b, 2 * jj, r:r + 1, :], stats[b, 2 * jj + 1, r:r + 1, :]], axis=1)
               for r in range(2)]
        s = dot(kk, qq, NT) * (scale * log2e) - row[0]
        if diagonal:
            col = lax.broadcasted_iota(jnp.int32, (1, 2 * R), 1)
            tq = (col % R) * 8 + (col // R + 2 * jj) * 2 + (c if j < 2 else 1 - c)
            rw = lax.broadcasted_iota(jnp.int32, (4 * R, 1), 0)
            tk = (rw % R) * 8 + (rw // R) * 2 + c
            s = jnp.where(tq >= tk, s, -jnp.inf)
        p = jnp.exp2(s)
        dp = dot(vv, dd, NT)
        dsb = (p * (dp - row[1])).astype(BF16)
        dv_acc[...] += dot(p.astype(BF16), dd)
        dk_acc[...] += dot(dsb, qq)
        g = dot(kt[...], dsb)
        if diagonal:
            dq[b, jj] = g
        else:
            dq[b, jj] += g

    @pl.loop(0, nc)
    def _(step):
        a = nc - 1 - step
        for i in range(3):
            data_in(a, i).wait_recv()
            stat_in(a, i).wait_recv()
        for zz in others:
            fwd(a, zz).start()
            fwd_stat(a, zz).start()
        dk_acc[...] = jnp.zeros_like(dk_acc)
        dv_acc[...] = jnp.zeros_like(dv_acc)
        kt[...] = G[a, :, 2].reshape(4 * R, D).T

        @pl.loop(a + 1, nc)
        def _(b):
            for j in range(4):
                tile(a, b, j, False)

            @pl.when(a == 0)
            def _():
                cross(b).start()

        for zz in range(4):
            fwd(a, zz).wait_recv()
            fwd_stat(a, zz).wait_recv()
        for j in range(4):
            tile(a, a, j, True)
        for zz in range(4):
            skv[a, zz, 0] = (dk_acc[zz * R:(zz + 1) * R, :] * scale).astype(BF16)
            skv[a, zz, 1] = dv_acc[zz * R:(zz + 1) * R, :].astype(BF16)
        for i in range(3):
            kv_out(a, i).start()
        kv_own(a).start()

    cross(0).start()

    @pl.loop(0, nc)
    def _(step):
        b = lax.rem(step + 1, nc)
        cross(b).wait_recv()
        for jj in range(2):
            tot = ((dqo[b, jj] + X[b, jj]) * scale).astype(BF16)
            sq[b, 2 * jj] = tot[:, :R]
            sq[b, 2 * jj + 1] = tot[:, R:]
        for i in range(3):
            q_out(b, i).start()
        q_own(b).start()

    @pl.loop(0, nc)
    def _(a):
        for i in range(3):
            data(a, i).wait_send()
            stat(a, i).wait_send()
            kv_out(a, i).wait_send()
            q_out(a, i).wait_send()
            kv_in(a, i).wait_recv()
            q_in(a, i).wait_recv()
        for zz in range(4):
            fwd(a, zz).wait_send()
            fwd_stat(a, zz).wait_send()
        kv_own(a).wait()
        q_own(a).wait()
        cross(a).wait_send()


def merge_kernel(okv, oq, dq, dk, dv, p2, p5):
    @pl.when(pl.program_id(0) == 0)
    def _():
        p2[...] = interleave(256, 4)
        p5[...] = interleave(512, 4)

    for t, out in ((0, dk), (1, dv)):
        for b in range(2):
            x = jnp.concatenate([okv[h, 0, t, b * 64:(b + 1) * 64, :] for h in range(4)], axis=0)
            out[b * 256:(b + 1) * 256, :] = dot(p2[...], x).astype(BF16)
    x = jnp.concatenate([oq[h, 0] for h in range(4)], axis=1)
    dq[...] = dot(p5[...], x, NT).astype(BF16)


def solution(mesh):
    rows = P(('dp', 'cp'))
    cols = P(None, ('dp', 'cp'))

    def local(q, k, v, o, do, lse):
        n, h, d = q.shape
        nc = n // R
        flat = [x.reshape(n * h, d) for x in (q, do, k, v, o)]
        any_ = pl.BlockSpec(memory_space=pl.ANY)
        sem = pltpu.SemaphoreType.DMA
        okv, oq = pl.pallas_call(
            functools.partial(exchange_kernel, nc),
            out_shape=(jax.ShapeDtypeStruct((4, nc, 2, R, D), BF16),
                       jax.ShapeDtypeStruct((4, nc, D, R), BF16)),
            in_specs=[any_] * 6,
            out_specs=(any_, any_),
            scratch_shapes=[pltpu.VMEM((n * h, d), BF16)] * 5 + [
                pltpu.VMEM((4, n), F32),
                pltpu.VMEM((256, 256), BF16),
                pltpu.VMEM((4, R, D), BF16),
                pltpu.VMEM((4, nc, 4, R, D), BF16),
                pltpu.VMEM((4, nc, 8, R), F32),
                pltpu.VMEM((nc, 4, 4, R, D), BF16),
                pltpu.VMEM((nc, 4, 8, R), F32),
                pltpu.VMEM((nc, 4, 2, R, D), BF16),
                pltpu.VMEM((nc, 4, 8, R), F32),
                pltpu.VMEM((D, 4 * R), BF16),
                pltpu.VMEM((4 * R, D), F32),
                pltpu.VMEM((4 * R, D), F32),
                pltpu.VMEM((nc, 2, D, 2 * R), F32),
                pltpu.VMEM((nc, 2, D, 2 * R), F32),
                pltpu.VMEM((nc, 2, D, 2 * R), F32),
                pltpu.VMEM((nc, 4, 2, R, D), BF16),
                pltpu.VMEM((nc, 4, D, R), BF16),
                sem((6,)),
            ] + [sem((nc, 4))] * 12 + [sem((nc,))] * 2,
            compiler_params=pltpu.CompilerParams(collective_id=0, has_side_effects=True,
                                                 vmem_limit_bytes=56 * 2 ** 20),
            name='exchange',
        )(*flat, lse)
        dq, dk, dv = pl.pallas_call(
            merge_kernel,
            grid=(nc,),
            out_shape=(jax.ShapeDtypeStruct((n * h, d), BF16),) * 3,
            in_specs=[pl.BlockSpec((4, 1, 2, R, D), lambda a: (0, a, 0, 0, 0)),
                      pl.BlockSpec((4, 1, D, R), lambda a: (0, a, 0, 0))],
            out_specs=(pl.BlockSpec((4 * R, D), lambda a: (a, 0)),) * 3,
            scratch_shapes=[pltpu.VMEM((256, 256), BF16), pltpu.VMEM((512, 512), BF16)],
            name='merge',
        )(okv, oq)
        return tuple(x.reshape(n, h, d) for x in (dq, dk, dv))

    return jax.shard_map(local, mesh=mesh,
                         in_specs=(rows, rows, rows, rows, rows, cols),
                         out_specs=(rows, rows, rows), check_vma=False)
```

time: 585 us -> 180 us (0.31); the launches traced: 577 us -> 180 us
  matrix products: 314 us -> 0 us
  waiting for transfers between devices: 186 us -> 0 us
  Pallas kernels: 0 us -> 179 us
  other arithmetic: 43.3 us -> 0 us
  local copies, waits for them, and re-layouts: 20.4 us -> 0 us
  starting transfers between devices: 12.2 us -> 0 us
    dot_general x40 -> x0, matrix products: 314 us -> none  [the longest x8 94.1 us: local(): jnp.einsum('kgij,ikgd->jkd', pr.astype(bf16), dos, preferred_element_type...]
    ppermute x30 -> x0, waiting for transfers between devices: 186 us -> none  [shift(): return lax.ppermute(x, 'cp', perm)]
    pallas_call x0 -> x2, Pallas kernels: none -> 179 us  [the longest x1 172 us: local(): pl.pallas_call(functools.partial(exchange_kernel, nc), out_shape=(jax.Sha...]
    add x17 -> x0, other arithmetic: 32.3 us -> none  [the longest x6 19.8 us: local(): dv + jnp.einsum('kgij,ikgd->jkd', pr.astype(bf16), dos, preferred_element...]
    unnamed x59 -> x0, local copies, waits for them, and re-layouts: 20.2 us -> none
    ppermute x30 -> x0, starting transfers between devices: 12.2 us -> none  [shift(): return lax.ppermute(x, 'cp', perm)]
    ge x1 -> x0, other arithmetic: 6.47 us -> none  [local(): mask = qpos >= jnp.arange(n)[None, :] * ncp + src]
  transfers between devices with their start and end apart: 30 -> 0, of which waited for: 12 -> 0; matrix products, arithmetic and copies ran while one was open for 63% -> 0% of each run, Pallas kernels for 0% -> 0%
where the time goes in v1:
time: 180 us
  Pallas kernels  179 us (99%)
    pallas_call x1, Pallas kernels, local(): pl.pallas_call(functools.partial(exchange_kernel, nc), out_shape=(jax.Sha...  172 us
    pallas_call x1, Pallas kernels, local(): pl.pallas_call(merge_kernel, grid=(nc,), out_shape=(jax.ShapeDtypeStruct(...  7.3 us

profile of v1, /device:TPU:0, one launch (start us, length us, event | category | flops | bytes accessed | tf_op | source)
XLA Modules:
  0.0 179.7 jit_solution(4989586914071404687)
XLA Ops:
  0.6 171.7 %exchange.1 = (bf16[4,8,2,128,128]{4,3,2,1,0:T(8,128)(2,1)}, bf16[4,8,128,128]{3,2,1,0:T(8,128)(2,1)}) custom-call(bf16[4096,128]{1,0:T(8,128)(2,1)} %bitcast.8, bf16[4096,128]{1,0:T(8,128)(2,1)} %bitcast.9, bf16[4096,128]{1,0:T(8,128)(2,1)} %bitcast.10, bf16[4096,128]{1,0:T(8,128)(2,1)} %bitcast.11, bf16[4096,128]{1,0:T(8,128)(2,1)} %bitcast.12, ...), custom_call_target="tpu_custom_call" | custom-call | tf_op jit(solution)/shard_map/exchange/pallas_call | solution.py:250
  172.4 7.3 %merge.1 = (bf16[4096,128]{1,0:T(8,128)(2,1)}, bf16[4096,128]{1,0:T(8,128)(2,1)}, bf16[4096,128]{1,0:T(8,128)(2,1)}) custom-call(bf16[4,8,2,128,128]{4,3,2,1,0:T(8,128)(2,1)} %get-tuple-element.8.okv, bf16[4,8,128,128]{3,2,1,0:T(8,128)(2,1)} %get-tuple-element.9.oq), custom_call_target="tpu_custom_call" | custom-call | tf_op jit(solution)/shard_map/merge/pallas_call | solution.py:280

commit v2 on v1

--- a/solution.py
+++ b/solution.py
@@ -34,10 +34,9 @@
     return jnp.where(r == (c % m) * heads + c // m, 1.0, 0.0).astype(BF16)
 
 
-def exchange_kernel(nc, q_h, do_h, k_h, v_h, o_h, lse_h, okv, oq,
-                    q_r, do_r, k_r, v_r, o_r, lse_r, perm, orel,
-                    sb, sbs, G, Gs, H, Hs, kt, dk_acc, dv_acc, dqo, dqp, X, skv, sq,
-                    lsem, ds, dr, ss, sr, fs, fr, gs, gr, ks, kr, qs, qr, xs, xr):
+def exchange_kernel(nc, q_h, do_h, k_h, v_h, o_h, lse_h, dq_o, dk_o, dv_o,
+                    q_r, do_r, k_r, v_r, o_r, lse_r, perm, iperm2, iperm4, orel,
+                    sb, sbs, G, Gs, H, Hs, kt, dk_acc, dv_acc, dqo, dqp, X, skv, sq, okv, oq, lse_sem, lsem, ds, dr, ss, sr, fs, fr, gs, gr, ks, kr, qs, qr, xs, xr):
     me = lax.axis_index('cp')
     z, c = me // 2, me % 2
     scale = D ** -0.5
@@ -46,18 +45,26 @@
     others = [lax.rem(z + i, 4) for i in (1, 2, 3)]
     home = [{'cp': zz * 2 + c} for zz in others]
 
-    loads = [pltpu.make_async_copy(s, d, lsem.at[i]) for i, (s, d) in enumerate(
-        ((q_h, q_r), (do_h, do_r), (k_h, k_r), (v_h, v_r), (o_h, o_r), (lse_h, lse_r)))]
-    for x in loads:
-        x.start()
-
+    def load(a, i):
+        s, d = ((q_h, q_r), (do_h, do_r), (k_h, k_r), (v_h, v_r), (o_h, o_r))[i]
+        rows = pl.ds(pl.multiple_of(a * 4 * R, 4 * R), 4 * R)
+        return pltpu.make_async_copy(s.at[rows], d.at[rows], lsem.at[a, i])
+
+    lse_load = pltpu.make_async_copy(lse_h, lse_r, lse_sem.at[0])
+    lse_load.start()
     barrier = pltpu.get_barrier_semaphore()
     for dev in home + [partner]:
         pl.semaphore_signal(barrier, inc=1, device_id=dev, device_id_type=MESH)
+
+    @pl.loop(0, nc)
+    def _(step):
+        for i in range(5):
+            load(nc - 1 - step, i).start()
+
     perm[...] = deinterleave(256, 4)
-    for x in loads:
-        x.wait()
-    pl.semaphore_wait(barrier, 4)
+    iperm2[...] = interleave(256, 4)
+    iperm4[...] = interleave(512, 4)
+    lse_load.wait()
 
     def remote(src, dst, ssem, rsem, dev):
         return pltpu.make_async_remote_copy(src_ref=src, dst_ref=dst, send_sem=ssem, recv_sem=rsem,
@@ -87,24 +94,18 @@
     def kv_in(a, i):
         return remote(skv.at[a, others[i]], okv.at[others[i], a], ks.at[a, others[i]], kr.at[a, others[i]], home[i])
 
-    def kv_own(a):
-        return pltpu.make_async_copy(skv.at[a, z], okv.at[z, a], ks.at[a, z])
-
     def q_out(a, i):
         return remote(sq.at[a, others[i]], oq.at[z, a], qs.at[a, others[i]], qr.at[a, z], home[i])
 
     def q_in(a, i):
         return remote(sq.at[a, others[i]], oq.at[others[i], a], qs.at[a, others[i]], qr.at[a, others[i]], home[i])
 
-    def q_own(a):
-        return pltpu.make_async_copy(sq.at[a, z], oq.at[z, a], qs.at[a, z])
-
     def cross(a):
         return remote(dqp.at[a], X.at[a], xs.at[a], xr.at[a], partner)
 
-    @pl.loop(0, nc)
-    def _(step):
-        a = nc - 1 - step
+    def relayout(a):
+        for i in range(5):
+            load(a, i).wait()
         pm = perm[...]
         for b in range(2):
             rows = pl.ds(pl.multiple_of(a * 512 + b * 256, 256), 256)
@@ -124,12 +125,24 @@
             sbs[h, a, 1:2, :] = delta
         G[a, z] = sb[z, a]
         Gs[a, z] = sbs[z, a]
+
+    def send(a):
         for i in range(3):
             data(a, i).start()
         for i in range(3):
             stat(a, i).start()
         fwd(a, z).start()
         fwd_stat(a, z).start()
+
+    relayout(nc - 1)
+    pl.semaphore_wait(barrier, 4)
+    send(nc - 1)
+
+    @pl.loop(1, nc)
+    def _(step):
+        a = nc - 1 - step
+        relayout(a)
+        send(a)
 
     def tile(a, b, j, diagonal):
         src, stats, dq = (G, Gs, dqo) if j < 2 else (H, Hs, dqp)
@@ -190,7 +203,6 @@
             skv[a, zz, 1] = dv_acc[zz * R:(zz + 1) * R, :].astype(BF16)
         for i in range(3):
             kv_out(a, i).start()
-        kv_own(a).start()
 
     cross(0).start()
 
@@ -204,7 +216,18 @@
             sq[b, 2 * jj + 1] = tot[:, R:]
         for i in range(3):
             q_out(b, i).start()
-        q_own(b).start()
+
+    @pl.loop(0, nc)
+    def _(step):
+        a = nc - 1 - step
+        for i in range(3):
+            kv_in(a, i).wait_recv()
+        okv[z, a] = skv[a, z]
+        for t in range(2):
+            for b in range(2):
+                x = jnp.concatenate([okv[h, a, t, b * 64:(b + 1) * 64, :] for h in range(4)], axis=0)
+                rows = pl.ds(pl.multiple_of(a * 4 * R + b * 256, 256), 256)
+                (dk_o, dv_o)[t][rows, :] = dot(iperm2[...], x).astype(BF16)
 
     @pl.loop(0, nc)
     def _(a):
@@ -212,29 +235,36 @@
             data(a, i).wait_send()
             stat(a, i).wait_send()
             kv_out(a, i).wait_send()
-            q_out(a, i).wait_send()
-            kv_in(a, i).wait_recv()
-            q_in(a, i).wait_recv()
         for zz in range(4):
             fwd(a, zz).wait_send()
             fwd_stat(a, zz).wait_send()
-        kv_own(a).wait()
-        q_own(a).wait()
         cross(a).wait_send()
 
-
-def merge_kernel(okv, oq, dq, dk, dv, p2, p5):
-    @pl.when(pl.program_id(0) == 0)
-    def _():
-        p2[...] = interleave(256, 4)
-        p5[...] = interleave(512, 4)
-
-    for t, out in ((0, dk), (1, dv)):
-        for b in range(2):
-            x = jnp.concatenate([okv[h, 0, t, b * 64:(b + 1) * 64, :] for h in range(4)], axis=0)
-            out[b * 256:(b + 1) * 256, :] = dot(p2[...], x).astype(BF16)
-    x = jnp.concatenate([oq[h, 0] for h in range(4)], axis=1)
-    dq[...] = dot(p5[...], x, NT).astype(BF16)
+    @pl.loop(0, nc)
+    def _(step):
+        b = lax.rem(step + 1, nc)
+        for i in range(3):
+            q_in(b, i).wait_recv()
+        oq[z, b] = sq[b, z]
+        x = jnp.concatenate([oq[h, b] for h in range(4)], axis=1)
+        rows = pl.ds(pl.multiple_of(b * 4 * R, 4 * R), 4 * R)
+        dq_o[rows, :] = dot(iperm4[...], x, NT).astype(BF16)
+
+    @pl.loop(0, nc)
+    def _(a):
+        for i in range(3):
+            q_out(a, i).wait_send()
+
+
+def place_kernel(*refs):
+    src, dst, sems = refs[:3], refs[3:6], refs[6]
+    n = src[0].shape[0] // 4
+    copies = [pltpu.make_async_copy(src[t].at[pl.ds(i * n, n)], dst[t].at[pl.ds(i * n, n)], sems.at[t, i])
+              for t in range(3) for i in range(4)]
+    for x in copies:
+        x.start()
+    for x in copies:
+        x.wait()
 
 
 def solution(mesh):
@@ -247,22 +277,24 @@
         flat = [x.reshape(n * h, d) for x in (q, do, k, v, o)]
         any_ = pl.BlockSpec(memory_space=pl.ANY)
         sem = pltpu.SemaphoreType.DMA
-        okv, oq = pl.pallas_call(
+        vmem = pl.BlockSpec(memory_space=pltpu.VMEM)
+        exchange = pl.pallas_call(
             functools.partial(exchange_kernel, nc),
-            out_shape=(jax.ShapeDtypeStruct((4, nc, 2, R, D), BF16),
-                       jax.ShapeDtypeStruct((4, nc, D, R), BF16)),
+            out_shape=(pltpu.VMEM((n * h, d), BF16),) * 3,
             in_specs=[any_] * 6,
-            out_specs=(any_, any_),
+            out_specs=(vmem,) * 3,
             scratch_shapes=[pltpu.VMEM((n * h, d), BF16)] * 5 + [
                 pltpu.VMEM((4, n), F32),
                 pltpu.VMEM((256, 256), BF16),
+                pltpu.VMEM((256, 256), BF16),
+                pltpu.VMEM((512, 512), BF16),
                 pltpu.VMEM((4, R, D), BF16),
                 pltpu.VMEM((4, nc, 4, R, D), BF16),
-                pltpu.VMEM((4, nc, 8, R), F32),
+                pltpu.VMEM((4, nc, 2, R), F32),
                 pltpu.VMEM((nc, 4, 4, R, D), BF16),
-                pltpu.VMEM((nc, 4, 8, R), F32),
+                pltpu.VMEM((nc, 4, 2, R), F32),
                 pltpu.VMEM((nc, 4, 2, R, D), BF16),
-                pltpu.VMEM((nc, 4, 8, R), F32),
+                pltpu.VMEM((nc, 4, 2, R), F32),
                 pltpu.VMEM((D, 4 * R), BF16),
                 pltpu.VMEM((4 * R, D), F32),
                 pltpu.VMEM((4 * R, D), F32),
@@ -271,22 +303,24 @@
                 pltpu.VMEM((nc, 2, D, 2 * R), F32),
                 pltpu.VMEM((nc, 4, 2, R, D), BF16),
                 pltpu.VMEM((nc, 4, D, R), BF16),
-                sem((6,)),
+                pltpu.VMEM((4, nc, 2, R, D), BF16),
+                pltpu.VMEM((4, nc, D, R), BF16),
+                sem((1,)), sem((nc, 5)),
             ] + [sem((nc, 4))] * 12 + [sem((nc,))] * 2,
             compiler_params=pltpu.CompilerParams(collective_id=0, has_side_effects=True,
                                                  vmem_limit_bytes=56 * 2 ** 20),
             name='exchange',
-        )(*flat, lse)
+        )
+        dq, dk, dv = exchange(*flat, lse)
+        outs = [pltpu.with_memory_space_constraint(x, pltpu.VMEM) for x in (dq, dk, dv)]
         dq, dk, dv = pl.pallas_call(
-            merge_kernel,
-            grid=(nc,),
+            place_kernel,
             out_shape=(jax.ShapeDtypeStruct((n * h, d), BF16),) * 3,
-            in_specs=[pl.BlockSpec((4, 1, 2, R, D), lambda a: (0, a, 0, 0, 0)),
-                      pl.BlockSpec((4, 1, D, R), lambda a: (0, a, 0, 0))],
-            out_specs=(pl.BlockSpec((4 * R, D), lambda a: (a, 0)),) * 3,
-            scratch_shapes=[pltpu.VMEM((256, 256), BF16), pltpu.VMEM((512, 512), BF16)],
-            name='merge',
-        )(okv, oq)
+            in_specs=[any_] * 3,
+            out_specs=(any_,) * 3,
+            scratch_shapes=[sem((3, 4))],
+            name='place',
+        )(*outs)
         return tuple(x.reshape(n, h, d) for x in (dq, dk, dv))
 
     return jax.shard_map(local, mesh=mesh,

time: 180 us -> 171 us (0.950)
  Pallas kernels: 179 us -> 171 us
    pallas_call x2, Pallas kernels: 179 us -> 171 us  [the longest x1 169 us: local(): dq, dk, dv = exchange(*flat, lse)]
where the time goes in v2:
time: 171 us
  Pallas kernels  171 us (100%)
    pallas_call x1, Pallas kernels, local(): dq, dk, dv = exchange(*flat, lse)  169 us

profile of v2, /device:TPU:0, one launch (start us, length us, event | category | flops | bytes accessed | tf_op | source)
XLA Modules:
  0.0 171.2 jit_solution(10020139330219614041)
XLA Ops:
  0.6 168.8 %exchange.1 = (bf16[4096,128]{1,0:T(8,128)(2,1)S(1)}, bf16[4096,128]{1,0:T(8,128)(2,1)S(1)}, bf16[4096,128]{1,0:T(8,128)(2,1)S(1)}) custom-call(bf16[4096,128]{1,0:T(8,128)(2,1)} %bitcast.8, bf16[4096,128]{1,0:T(8,128)(2,1)} %bitcast.9, bf16[4096,128]{1,0:T(8,128)(2,1)} %bitcast.10, bf16[4096,128]{1,0:T(8,128)(2,1)} %bitcast.11, bf16[4096,128]{1,0:T(8,128)(2,1)} %bitcast.12, ...), custom_call_target="tpu_custom_call" | custom-call | tf_op jit(solution)/shard_map/exchange/pallas_call | solution.py:314
  169.4 1.8 %place.1 = (bf16[4096,128]{1,0:T(8,128)(2,1)}, bf16[4096,128]{1,0:T(8,128)(2,1)}, bf16[4096,128]{1,0:T(8,128)(2,1)}) custom-call(bf16[4096,128]{1,0:T(8,128)(2,1)S(1)} %get-tuple-element.9.refs_0_, bf16[4096,128]{1,0:T(8,128)(2,1)S(1)} %get-tuple-element.10.refs_1_, bf16[4096,128]{1,0:T(8,128)(2,1)S(1)} %get-tuple-element.11.refs_2_), custom_call_target="tpu_custom_call" | custom-call | tf_op jit(solution)/shard_map/place/pallas_call | solution.py:316

commit v3 on v2

--- a/solution.py
+++ b/solution.py
@@ -42,7 +42,10 @@
     scale = D ** -0.5
     log2e = math.log2(math.e)
     partner = {'cp': z * 2 + (1 - c)}
-    others = [lax.rem(z + i, 4) for i in (1, 2, 3)]
+    near, far = z + 1 - 2 * (z % 2), 3 * (1 - z // 2)
+    others = [near + c * (far - near), 6 - z - near - far, far + c * (near - far)]
+    half = nc // 2
+    group = (pl.ds(nc - 1, 1), pl.ds(0, nc - 1))
     home = [{'cp': zz * 2 + c} for zz in others]
 
     def load(a, i):
@@ -62,8 +65,6 @@
             load(nc - 1 - step, i).start()
 
     perm[...] = deinterleave(256, 4)
-    iperm2[...] = interleave(256, 4)
-    iperm4[...] = interleave(512, 4)
     lse_load.wait()
 
     def remote(src, dst, ssem, rsem, dev):
@@ -73,32 +74,41 @@
     def data(a, i):
         return remote(sb.at[others[i], a], G.at[a, z], ds.at[a, others[i]], dr.at[a, z], home[i])
 
-    def stat(a, i):
-        return remote(sbs.at[others[i], a], Gs.at[a, z], ss.at[a, others[i]], sr.at[a, z], home[i])
+    def stat(g, i):
+        return remote(sbs.at[others[i], group[g]], Gs.at[z, group[g]],
+                      ss.at[g, others[i]], sr.at[g, z], home[i])
 
     def data_in(a, i):
         return remote(sb.at[others[i], a], G.at[a, others[i]], ds.at[a, others[i]], dr.at[a, others[i]], home[i])
 
-    def stat_in(a, i):
-        return remote(sbs.at[others[i], a], Gs.at[a, others[i]], ss.at[a, others[i]], sr.at[a, others[i]], home[i])
+    def stat_in(g, i):
+        return remote(sbs.at[others[i], group[g]], Gs.at[others[i], group[g]],
+                      ss.at[g, others[i]], sr.at[g, others[i]], home[i])
 
     def fwd(a, zz):
         return remote(G.at[a, zz, pl.ds(0, 2)], H.at[a, zz], fs.at[a, zz], fr.at[a, zz], partner)
 
-    def fwd_stat(a, zz):
-        return remote(Gs.at[a, zz], Hs.at[a, zz], gs.at[a, zz], gr.at[a, zz], partner)
-
-    def kv_out(a, i):
-        return remote(skv.at[a, others[i]], okv.at[z, a], ks.at[a, others[i]], kr.at[a, z], home[i])
-
-    def kv_in(a, i):
-        return remote(skv.at[a, others[i]], okv.at[others[i], a], ks.at[a, others[i]], kr.at[a, others[i]], home[i])
-
-    def q_out(a, i):
-        return remote(sq.at[a, others[i]], oq.at[z, a], qs.at[a, others[i]], qr.at[a, z], home[i])
-
-    def q_in(a, i):
-        return remote(sq.at[a, others[i]], oq.at[others[i], a], qs.at[a, others[i]], qr.at[a, others[i]], home[i])
+    def fwd_stat(g, zz):
+        return remote(Gs.at[zz, group[g]], Hs.at[zz, group[g]], gs.at[g, zz], gr.at[g, zz], partner)
+
+    def pair(p):
+        return pl.ds(2 * p, 2)
+
+    def kv_out(p, i):
+        return remote(skv.at[others[i], pair(p)], okv.at[z, pair(p)],
+                      ks.at[p, others[i]], kr.at[p, z], home[i])
+
+    def kv_in(p, i):
+        return remote(skv.at[others[i], pair(p)], okv.at[others[i], pair(p)],
+                      ks.at[p, others[i]], kr.at[p, others[i]], home[i])
+
+    def q_out(p, i):
+        return remote(sq.at[others[i], pair(p)], oq.at[z, pair(p)],
+                      qs.at[p, others[i]], qr.at[p, z], home[i])
+
+    def q_in(p, i):
+        return remote(sq.at[others[i], pair(p)], oq.at[others[i], pair(p)],
+                      qs.at[p, others[i]], qr.at[p, others[i]], home[i])
 
     def cross(a):
         return remote(dqp.at[a], X.at[a], xs.at[a], xr.at[a], partner)
@@ -124,25 +134,35 @@
             sbs[h, a, 0:1, :] = lse_r[h:h + 1, pl.ds(pl.multiple_of(a * R, R), R)] * log2e
             sbs[h, a, 1:2, :] = delta
         G[a, z] = sb[z, a]
-        Gs[a, z] = sbs[z, a]
+        Gs[z, a] = sbs[z, a]
 
     def send(a):
         for i in range(3):
             data(a, i).start()
-        for i in range(3):
-            stat(a, i).start()
         fwd(a, z).start()
-        fwd_stat(a, z).start()
+
+    def send_stats(g):
+        for i in range(3):
+            stat(g, i).start()
+        fwd_stat(g, z).start()
 
     relayout(nc - 1)
     pl.semaphore_wait(barrier, 4)
     send(nc - 1)
+    send_stats(0)
 
     @pl.loop(1, nc)
     def _(step):
-        a = nc - 1 - step
-        relayout(a)
-        send(a)
+        relayout(nc - 1 - step)
+
+    send_stats(1)
+
+    @pl.loop(1, nc)
+    def _(step):
+        send(nc - 1 - step)
+
+    iperm2[...] = interleave(256, 4)
+    iperm4[...] = interleave(512, 4)
 
     def tile(a, b, j, diagonal):
         src, stats, dq = (G, Gs, dqo) if j < 2 else (H, Hs, dqp)
@@ -151,7 +171,7 @@
         vv = G[a, :, 3].reshape(4 * R, D)
         qq = src[b, 2 * jj:2 * jj + 2, 0].reshape(2 * R, D)
         dd = src[b, 2 * jj:2 * jj + 2, 1].reshape(2 * R, D)
-        row = [jnp.concatenate([stats[b, 2 * jj, r:r + 1, :], stats[b, 2 * jj + 1, r:r + 1, :]], axis=1)
+        row = [jnp.concatenate([stats[2 * jj, b, r:r + 1, :], stats[2 * jj + 1, b, r:r + 1, :]], axis=1)
                for r in range(2)]
         s = dot(kk, qq, NT) * (scale * log2e) - row[0]
         if diagonal:
@@ -176,10 +196,15 @@
         a = nc - 1 - step
         for i in range(3):
             data_in(a, i).wait_recv()
-            stat_in(a, i).wait_recv()
         for zz in others:
             fwd(a, zz).start()
-            fwd_stat(a, zz).start()
+        for g in range(2):
+            @pl.when(step == g)
+            def _():
+                for i in range(3):
+                    stat_in(g, i).wait_recv()
+                for zz in others:
+                    fwd_stat(g, zz).start()
         dk_acc[...] = jnp.zeros_like(dk_acc)
         dv_acc[...] = jnp.zeros_like(dv_acc)
         kt[...] = G[a, :, 2].reshape(4 * R, D).T
@@ -195,65 +220,82 @@
 
         for zz in range(4):
             fwd(a, zz).wait_recv()
-            fwd_stat(a, zz).wait_recv()
+        for g in range(2):
+            @pl.when(step == g)
+            def _():
+                for zz in range(4):
+                    fwd_stat(g, zz).wait_recv()
         for j in range(4):
             tile(a, a, j, True)
         for zz in range(4):
-            skv[a, zz, 0] = (dk_acc[zz * R:(zz + 1) * R, :] * scale).astype(BF16)
-            skv[a, zz, 1] = dv_acc[zz * R:(zz + 1) * R, :].astype(BF16)
-        for i in range(3):
-            kv_out(a, i).start()
+            skv[zz, a, 0] = (dk_acc[zz * R:(zz + 1) * R, :] * scale).astype(BF16)
+            skv[zz, a, 1] = dv_acc[zz * R:(zz + 1) * R, :].astype(BF16)
+
+        @pl.when(a % 2 == 0)
+        def _():
+            for i in range(3):
+                kv_out(a // 2, i).start()
 
     cross(0).start()
 
-    @pl.loop(0, nc)
-    def _(step):
-        b = lax.rem(step + 1, nc)
-        cross(b).wait_recv()
-        for jj in range(2):
-            tot = ((dqo[b, jj] + X[b, jj]) * scale).astype(BF16)
-            sq[b, 2 * jj] = tot[:, :R]
-            sq[b, 2 * jj + 1] = tot[:, R:]
-        for i in range(3):
-            q_out(b, i).start()
-
-    @pl.loop(0, nc)
-    def _(step):
-        a = nc - 1 - step
-        for i in range(3):
-            kv_in(a, i).wait_recv()
-        okv[z, a] = skv[a, z]
-        for t in range(2):
-            for b in range(2):
-                x = jnp.concatenate([okv[h, a, t, b * 64:(b + 1) * 64, :] for h in range(4)], axis=0)
-                rows = pl.ds(pl.multiple_of(a * 4 * R + b * 256, 256), 256)
-                (dk_o, dv_o)[t][rows, :] = dot(iperm2[...], x).astype(BF16)
+    @pl.loop(0, half)
+    def _(step):
+        p = lax.rem(step + 1, half)
+        for e in range(2):
+            b = 2 * p + e
+            cross(b).wait_recv()
+            for jj in range(2):
+                tot = ((dqo[b, jj] + X[b, jj]) * scale).astype(BF16)
+                sq[2 * jj, b] = tot[:, :R]
+                sq[2 * jj + 1, b] = tot[:, R:]
+        for i in range(3):
+            q_out(p, i).start()
+
+    @pl.loop(0, half)
+    def _(step):
+        p = half - 1 - step
+        for i in range(3):
+            kv_in(p, i).wait_recv()
+        for e in range(2):
+            a = 2 * p + e
+            okv[z, a] = skv[z, a]
+            for t in range(2):
+                for b in range(2):
+                    x = jnp.concatenate([okv[h, a, t, b * 64:(b + 1) * 64, :] for h in range(4)], axis=0)
+                    rows = pl.ds(pl.multiple_of(a * 4 * R + b * 256, 256), 256)
+                    (dk_o, dv_o)[t][rows, :] = dot(iperm2[...], x).astype(BF16)
 
     @pl.loop(0, nc)
     def _(a):
         for i in range(3):
             data(a, i).wait_send()
-            stat(a, i).wait_send()
-            kv_out(a, i).wait_send()
         for zz in range(4):
             fwd(a, zz).wait_send()
-            fwd_stat(a, zz).wait_send()
         cross(a).wait_send()
 
-    @pl.loop(0, nc)
-    def _(step):
-        b = lax.rem(step + 1, nc)
-        for i in range(3):
-            q_in(b, i).wait_recv()
-        oq[z, b] = sq[b, z]
-        x = jnp.concatenate([oq[h, b] for h in range(4)], axis=1)
-        rows = pl.ds(pl.multiple_of(b * 4 * R, 4 * R), 4 * R)
-        dq_o[rows, :] = dot(iperm4[...], x, NT).astype(BF16)
-
-    @pl.loop(0, nc)
-    def _(a):
-        for i in range(3):
-            q_out(a, i).wait_send()
+    for g in range(2):
+        for i in range(3):
+            stat(g, i).wait_send()
+        for zz in range(4):
+            fwd_stat(g, zz).wait_send()
+
+    @pl.loop(0, half)
+    def _(step):
+        p = lax.rem(step + 1, half)
+        for i in range(3):
+            kv_out(p, i).wait_send()
+            q_in(p, i).wait_recv()
+        for e in range(2):
+            b = 2 * p + e
+            oq[z, b] = sq[z, b]
+            x = jnp.concatenate([oq[h, b] for h in range(4)], axis=1)
+            rows = pl.ds(pl.multiple_of(b * 4 * R, 4 * R), 4 * R)
+            dq_o[rows, :] = dot(iperm4[...], x, NT).astype(BF16)
+
+    @pl.loop(0, half)
+    def _(p):
+        for i in range(3):
+            q_out(p, i).wait_send()
 
 
 def place_kernel(*refs):
@@ -292,21 +334,22 @@
                 pltpu.VMEM((4, nc, 4, R, D), BF16),
                 pltpu.VMEM((4, nc, 2, R), F32),
                 pltpu.VMEM((nc, 4, 4, R, D), BF16),
-                pltpu.VMEM((nc, 4, 2, R), F32),
+                pltpu.VMEM((4, nc, 2, R), F32),
                 pltpu.VMEM((nc, 4, 2, R, D), BF16),
-                pltpu.VMEM((nc, 4, 2, R), F32),
+                pltpu.VMEM((4, nc, 2, R), F32),
                 pltpu.VMEM((D, 4 * R), BF16),
                 pltpu.VMEM((4 * R, D), F32),
                 pltpu.VMEM((4 * R, D), F32),
                 pltpu.VMEM((nc, 2, D, 2 * R), F32),
                 pltpu.VMEM((nc, 2, D, 2 * R), F32),
                 pltpu.VMEM((nc, 2, D, 2 * R), F32),
-                pltpu.VMEM((nc, 4, 2, R, D), BF16),
-                pltpu.VMEM((nc, 4, D, R), BF16),
+                pltpu.VMEM((4, nc, 2, R, D), BF16),
+                pltpu.VMEM((4, nc, D, R), BF16),
                 pltpu.VMEM((4, nc, 2, R, D), BF16),
                 pltpu.VMEM((4, nc, D, R), BF16),
                 sem((1,)), sem((nc, 5)),
-            ] + [sem((nc, 4))] * 12 + [sem((nc,))] * 2,
+            ] + [sem((nc, 4))] * 2 + [sem((2, 4))] * 2 + [sem((nc, 4))] * 2 + [sem((2, 4))] * 2 + [
+                sem((nc // 2, 4))] * 4 + [sem((nc,))] * 2,
             compiler_params=pltpu.CompilerParams(collective_id=0, has_side_effects=True,
                                                  vmem_limit_bytes=56 * 2 ** 20),
             name='exchange',

time: 171 us -> 170 us (level)
  no operation moved by 1% of the time
where the time goes in v3:
time: 170 us
  Pallas kernels  170 us (100%)
    pallas_call x1, Pallas kernels, local(): dq, dk, dv = exchange(*flat, lse)  168 us

profile of v3, /device:TPU:0, one launch (start us, length us, event | category | flops | bytes accessed | tf_op | source)
XLA Modules:
  0.0 170.2 jit_solution(11772566080492348550)
XLA Ops:
  0.6 167.8 %exchange.1 = (bf16[4096,128]{1,0:T(8,128)(2,1)S(1)}, bf16[4096,128]{1,0:T(8,128)(2,1)S(1)}, bf16[4096,128]{1,0:T(8,128)(2,1)S(1)}) custom-call(bf16[4096,128]{1,0:T(8,128)(2,1)} %bitcast.8, bf16[4096,128]{1,0:T(8,128)(2,1)} %bitcast.9, bf16[4096,128]{1,0:T(8,128)(2,1)} %bitcast.10, bf16[4096,128]{1,0:T(8,128)(2,1)} %bitcast.11, bf16[4096,128]{1,0:T(8,128)(2,1)} %bitcast.12, ...), custom_call_target="tpu_custom_call" | custom-call | tf_op jit(solution)/shard_map/exchange/pallas_call | solution.py:357
  168.4 1.8 %place.1 = (bf16[4096,128]{1,0:T(8,128)(2,1)}, bf16[4096,128]{1,0:T(8,128)(2,1)}, bf16[4096,128]{1,0:T(8,128)(2,1)}) custom-call(bf16[4096,128]{1,0:T(8,128)(2,1)S(1)} %get-tuple-element.9.refs_0_, bf16[4096,128]{1,0:T(8,128)(2,1)S(1)} %get-tuple-element.10.refs_1_, bf16[4096,128]{1,0:T(8,128)(2,1)S(1)} %get-tuple-element.11.refs_2_), custom_call_target="tpu_custom_call" | custom-call | tf_op jit(solution)/shard_map/place/pallas_call | solution.py:359

commit v4 on v3

--- a/solution.py
+++ b/solution.py
@@ -47,6 +47,8 @@
     half = nc // 2
     group = (pl.ds(nc - 1, 1), pl.ds(0, nc - 1))
     home = [{'cp': zz * 2 + c} for zz in others]
+    q_to = [far, 6 - z - near - far, near]
+    q_home = [{'cp': zz * 2 + c} for zz in q_to]
 
     def load(a, i):
         s, d = ((q_h, q_r), (do_h, do_r), (k_h, k_r), (v_h, v_r), (o_h, o_r))[i]
@@ -102,13 +104,13 @@
         return remote(skv.at[others[i], pair(p)], okv.at[others[i], pair(p)],
                       ks.at[p, others[i]], kr.at[p, others[i]], home[i])
 
-    def q_out(p, i):
-        return remote(sq.at[others[i], pair(p)], oq.at[z, pair(p)],
-                      qs.at[p, others[i]], qr.at[p, z], home[i])
-
-    def q_in(p, i):
-        return remote(sq.at[others[i], pair(p)], oq.at[others[i], pair(p)],
-                      qs.at[p, others[i]], qr.at[p, others[i]], home[i])
+    def q_out(sl, k, i):
+        return remote(sq.at[q_to[i], sl], oq.at[z, sl], qs.at[k, q_to[i]], qr.at[k, z], q_home[i])
+
+    def q_in(sl, k, i):
+        return remote(sq.at[q_to[i], sl], oq.at[q_to[i], sl], qs.at[k, q_to[i]], qr.at[k, q_to[i]], q_home[i])
+
+    last = ((1, pl.ds(1, 1), 0), (0, pl.ds(0, 1), half))
 
     def cross(a):
         return remote(dqp.at[a], X.at[a], xs.at[a], xr.at[a], partner)
@@ -238,18 +240,24 @@
 
     cross(0).start()
 
-    @pl.loop(0, half)
-    def _(step):
-        p = lax.rem(step + 1, half)
-        for e in range(2):
-            b = 2 * p + e
-            cross(b).wait_recv()
-            for jj in range(2):
-                tot = ((dqo[b, jj] + X[b, jj]) * scale).astype(BF16)
-                sq[2 * jj, b] = tot[:, :R]
-                sq[2 * jj + 1, b] = tot[:, R:]
-        for i in range(3):
-            q_out(p, i).start()
+    def finish(b):
+        cross(b).wait_recv()
+        for jj in range(2):
+            tot = ((dqo[b, jj] + X[b, jj]) * scale).astype(BF16)
+            sq[2 * jj, b] = tot[:, :R]
+            sq[2 * jj + 1, b] = tot[:, R:]
+
+    @pl.loop(1, half)
+    def _(p):
+        finish(2 * p)
+        finish(2 * p + 1)
+        for i in range(3):
+            q_out(pair(p), p, i).start()
+
+    for b, sl, k in last:
+        finish(b)
+        for i in range(3):
+            q_out(sl, k, i).start()
 
     @pl.loop(0, half)
     def _(step):
@@ -279,23 +287,32 @@
         for zz in range(4):
             fwd_stat(g, zz).wait_send()
 
-    @pl.loop(0, half)
-    def _(step):
-        p = lax.rem(step + 1, half)
-        for i in range(3):
-            kv_out(p, i).wait_send()
-            q_in(p, i).wait_recv()
-        for e in range(2):
-            b = 2 * p + e
-            oq[z, b] = sq[z, b]
-            x = jnp.concatenate([oq[h, b] for h in range(4)], axis=1)
-            rows = pl.ds(pl.multiple_of(b * 4 * R, 4 * R), 4 * R)
-            dq_o[rows, :] = dot(iperm4[...], x, NT).astype(BF16)
+    def merge_q(b):
+        oq[z, b] = sq[z, b]
+        x = jnp.concatenate([oq[h, b] for h in range(4)], axis=1)
+        rows = pl.ds(pl.multiple_of(b * 4 * R, 4 * R), 4 * R)
+        dq_o[rows, :] = dot(iperm4[...], x, NT).astype(BF16)
 
     @pl.loop(0, half)
     def _(p):
         for i in range(3):
-            q_out(p, i).wait_send()
+            kv_out(p, i).wait_send()
+
+    @pl.loop(1, half)
+    def _(p):
+        for i in range(3):
+            q_out(pair(p), p, i).wait_send()
+            q_in(pair(p), p, i).wait_recv()
+        merge_q(2 * p)
+        merge_q(2 * p + 1)
+
+    for b, sl, k in last:
+        for i in range(3):
+            q_in(sl, k, i).wait_recv()
+        merge_q(b)
+    for b, sl, k in last:
+        for i in range(3):
+            q_out(sl, k, i).wait_send()
 
 
 def place_kernel(*refs):
@@ -349,7 +366,7 @@
                 pltpu.VMEM((4, nc, D, R), BF16),
                 sem((1,)), sem((nc, 5)),
             ] + [sem((nc, 4))] * 2 + [sem((2, 4))] * 2 + [sem((nc, 4))] * 2 + [sem((2, 4))] * 2 + [
-                sem((nc // 2, 4))] * 4 + [sem((nc,))] * 2,
+                sem((nc // 2, 4))] * 2 + [sem((nc // 2 + 1, 4))] * 2 + [sem((nc,))] * 2,
             compiler_params=pltpu.CompilerParams(collective_id=0, has_side_effects=True,
                                                  vmem_limit_bytes=56 * 2 ** 20),
             name='exchange',

time: 170 us -> 170 us (level)
  no operation moved by 1% of the time
where the time goes in v4:
time: 170 us; the launch traced here: 169 us
  Pallas kernels  169 us (99%)
    pallas_call x1, Pallas kernels, local(): dq, dk, dv = exchange(*flat, lse)  167 us

profile of v4, /device:TPU:0, one launch (start us, length us, event | category | flops | bytes accessed | tf_op | source)
XLA Modules:
  0.0 169.4 jit_solution(18112536365441479181)
XLA Ops:
  0.6 167.0 %exchange.1 = (bf16[4096,128]{1,0:T(8,128)(2,1)S(1)}, bf16[4096,128]{1,0:T(8,128)(2,1)S(1)}, bf16[4096,128]{1,0:T(8,128)(2,1)S(1)}) custom-call(bf16[4096,128]{1,0:T(8,128)(2,1)} %bitcast.8, bf16[4096,128]{1,0:T(8,128)(2,1)} %bitcast.9, bf16[4096,128]{1,0:T(8,128)(2,1)} %bitcast.10, bf16[4096,128]{1,0:T(8,128)(2,1)} %bitcast.11, bf16[4096,128]{1,0:T(8,128)(2,1)} %bitcast.12, ...), custom_call_target="tpu_custom_call" | custom-call | tf_op jit(solution)/shard_map/exchange/pallas_call | solution.py:374
  167.6 1.8 %place.1 = (bf16[4096,128]{1,0:T(8,128)(2,1)}, bf16[4096,128]{1,0:T(8,128)(2,1)}, bf16[4096,128]{1,0:T(8,128)(2,1)}) custom-call(bf16[4096,128]{1,0:T(8,128)(2,1)S(1)} %get-tuple-element.9.refs_0_, bf16[4096,128]{1,0:T(8,128)(2,1)S(1)} %get-tuple-element.10.refs_1_, bf16[4096,128]{1,0:T(8,128)(2,1)S(1)} %get-tuple-element.11.refs_2_), custom_call_target="tpu_custom_call" | custom-call | tf_op jit(solution)/shard_map/place/pallas_call | solution.py:376
